TPU v7x, 256 devices: a whole 4x4x8 slice. The times are simulated.
256 devices in a mesh: dp: 64 (over y, x, z_lo, core), mp: 4 (over z_hi).
Axes of the slice: x: 4, y: 4, z: 8 (z_hi: 4, z_lo: 2; z = z_hi * 2 + z_lo), core: 2. Of those that a mesh axis runs over, the one named last changes fastest.
Arguments:
- feature_ids: int32 [64, 16384, 8], P('dp'), may hold values from 0 to 4095
- tables: bfloat16 [64, 4096, 128], P('dp'), may hold values from -5 to 5
- table_of_feature: int32 [64], replicated, may hold values from 0 to 63, each once
- cross_down: bfloat16 [2, 8192, 512], P(None, 'mp'), may hold values from -0.0625 to 0.0625
- cross_up: bfloat16 [2, 8192, 512], P(None, 'mp'), may hold values from -0.125 to 0.125
- cross_bias: float32 [2, 8192], P(None, 'mp'), may hold values from -3 to 3
- tower_weight: bfloat16 [8192, 2048], P('dp', 'mp'), may hold values from -0.0625 to 0.0625
- tower_bias: float32 [2048], P('mp'), may hold values from -3 to 3
Outputs:
- hidden: bfloat16 [16384, 2048], P('dp', 'mp')
Inputs may be any that keep to these rules, and one draw needn't show every extreme that they name: `feature_ids`: each id indexes a row of its own table. `table_of_feature`: each table serves exactly one feature.
All inputs are finite; a program needn't handle non-finite values.
Results may differ from a plain program's by a relative error of at most 0.015.
Values may be sent and summed in bfloat16 or wider, within the bound.
A program may use at most 64 MiB of HBM per device.

v0:
```python
import jax
import jax.numpy as jnp
from jax import lax
from jax.sharding import PartitionSpec as P


def from_everyone(x, axis):
    length = lax.axis_size(axis)
    return lax.all_to_all(jnp.broadcast_to(x[None], (length, *x.shape)), axis, 0, 0, tiled=True)


def taken_together(x, axis):
    everything = from_everyone(x, axis)
    return jnp.sum(everything.astype(jnp.float32), axis=0)


def body(
    feature_ids,
    tables,
    table_of_feature,
    cross_down,
    cross_up,
    cross_bias,
    tower_weight,
    tower_bias,
):
    groups = lax.axis_size("dp")
    members = lax.axis_size("mp")
    member = lax.axis_index("mp")
    table_count, batch_size, hot_count = feature_ids.shape
    row_count = batch_size // (groups * members)
    shaped = feature_ids[0].reshape(groups, members, row_count, hot_count)
    own_ids = lax.dynamic_index_in_dim(shaped, member, 1, keepdims=False).reshape(
        groups * row_count, hot_count
    )
    summed = jnp.zeros((groups * row_count, tables.shape[2]), jnp.float32)
    for hot_index in range(hot_count):
        summed = summed + jnp.take(tables[0], own_ids[:, hot_index], axis=0).astype(jnp.float32)
    columns = [summed.astype(jnp.bfloat16)]
    pooled = jnp.stack(columns, axis=1)
    regrouped = lax.all_to_all(pooled, "dp", split_axis=0, concat_axis=1, tiled=True)
    ordered = jnp.take(regrouped, table_of_feature, axis=1)
    by_width = lax.all_to_all(ordered, "mp", split_axis=1, concat_axis=0, tiled=True)
    group_rows = by_width.shape[0]
    embedded = by_width.reshape(group_rows, -1)
    embedded_wide = embedded.astype(jnp.float32)
    crossed = embedded
    layer_total = cross_down.shape[0]
    for layer_index in range(layer_total):
        partial_value = jnp.dot(
            crossed, cross_down[layer_index], preferred_element_type=jnp.float32
        )
        projected = (
            taken_together(partial_value.astype(jnp.bfloat16), "mp")
            .astype(jnp.float32)
            .astype(jnp.bfloat16)
        )
        lifted = lax.dot_general(
            projected,
            cross_up[layer_index],
            (((1,), (1,)), ((), ())),
            preferred_element_type=jnp.float32,
        )
        crossed = (
            embedded_wide * (lifted + cross_bias[layer_index]) + crossed.astype(jnp.float32)
        ).astype(jnp.bfloat16)
    full_rows = lax.all_gather(crossed, "mp", axis=1, tiled=True)
    pre_act = jnp.dot(
        full_rows,
        lax.all_gather(tower_weight, "dp", axis=0, tiled=True),
        preferred_element_type=jnp.float32,
    )
    return jax.nn.relu(pre_act + tower_bias).astype(jnp.bfloat16)


def solution(mesh):
    return jax.shard_map(
        body,
        mesh=mesh,
        in_specs=(
            P("dp", None, None),
            P("dp", None, None),
            P(),
            P(None, "mp", None),
            P(None, "mp", None),
            P(None, "mp"),
            P("dp", "mp"),
            P("mp"),
        ),
        out_specs=P("dp", "mp"),
        check_vma=False,
    )
```

profile of v0, /device:TPU:2, one launch (start us, length us, event | category | flops | bytes accessed | tf_op | source)
XLA Modules:
  0.0 485.6 jit_solution(10441669731089742331)
XLA Ops:
  6.5 1.8 reshape_squeeze.3
  9.6 12.1 %gather_fusion.2 = bf16[4096,128]{1,0:T(8,128)(2,1)S(1)} fusion(bf16[4096,128]{1,0:T(8,128)(2,1)S(1)} %bitcast.56, s32[4096]{0:T(1024)S(1)} %fusion.26), kind=kCustom, calls=%fused_computation.1.clone | custom fusion | bytes 2113536 | tf_op jit(solution)/shard_map/jit(_take)/gather | solution.py:38
  21.7 12.1 %gather_fusion.3 = bf16[4096,128]{1,0:T(8,128)(2,1)S(1)} fusion(bf16[4096,128]{1,0:T(8,128)(2,1)S(1)} %bitcast.57, s32[4096]{0:T(1024)S(1)} %fusion.27), kind=kCustom, calls=%fused_computation.2.clone | custom fusion | bytes 2113536 | tf_op jit(solution)/shard_map/jit(_take)/gather | solution.py:38
  33.9 14.9 %gather_fusion.4 = bf16[4096,128]{1,0:T(8,128)(2,1)} fusion(bf16[4096,128]{1,0:T(8,128)(2,1)S(1)} %bitcast.58, s32[4096]{0:T(1024)S(1)} %fusion.28), kind=kCustom, calls=%fused_computation.3.clone | custom fusion | bytes 2113536 | tf_op jit(solution)/shard_map/jit(_take)/gather | solution.py:38
  48.8 14.9 %gather_fusion.5 = bf16[4096,128]{1,0:T(8,128)(2,1)} fusion(bf16[4096,128]{1,0:T(8,128)(2,1)S(1)} %bitcast.59, s32[4096]{0:T(1024)S(1)} %fusion.29), kind=kCustom, calls=%fused_computation.4.clone | custom fusion | bytes 2113536 | tf_op jit(solution)/shard_map/jit(_take)/gather | solution.py:38
  63.6 14.9 %gather_fusion.6 = bf16[4096,128]{1,0:T(8,128)(2,1)} fusion(bf16[4096,128]{1,0:T(8,128)(2,1)S(1)} %bitcast.60, s32[4096]{0:T(1024)S(1)} %fusion.30), kind=kCustom, calls=%fused_computation.5.clone | custom fusion | bytes 2113536 | tf_op jit(solution)/shard_map/jit(_take)/gather | solution.py:38
  78.5 14.9 %gather_fusion.7 = bf16[4096,128]{1,0:T(8,128)(2,1)} fusion(bf16[4096,128]{1,0:T(8,128)(2,1)S(1)} %bitcast.61, s32[4096]{0:T(1024)S(1)} %fusion.31), kind=kCustom, calls=%fused_computation.6.clone | custom fusion | bytes 2113536 | tf_op jit(solution)/shard_map/jit(_take)/gather | solution.py:38
  93.4 14.9 %gather_fusion.8 = bf16[4096,128]{1,0:T(8,128)(2,1)} fusion(bf16[4096,128]{1,0:T(8,128)(2,1)S(1)} %bitcast.62, s32[4096]{0:T(1024)S(1)} %fusion.32), kind=kCustom, calls=%fused_computation.7.clone | custom fusion | bytes 2113536 | tf_op jit(solution)/shard_map/jit(_take)/gather | solution.py:38
  108.3 14.9 %gather_fusion.1 = bf16[4096,128]{1,0:T(8,128)(2,1)} fusion(bf16[4096,128]{1,0:T(8,128)(2,1)S(1)} %bitcast.55, s32[4096]{0:T(1024)S(1)} %fusion.25), kind=kCustom, calls=%fused_computation.clone | custom fusion | bytes 2113536 | tf_op jit(solution)/shard_map/jit(_take)/gather | solution.py:38
  123.2 9.9 %fusion.22 = bf16[4096,1,128]{2,0,1:T(8,128)(2,1)} fusion(bf16[4096,128]{1,0:T(8,128)(2,1)} %gather_fusion.8, bf16[4096,128]{1,0:T(8,128)(2,1)} %gather_fusion.7, bf16[4096,128]{1,0:T(8,128)(2,1)} %gather_fusion.6, bf16[4096,128]{1,0:T(8,128)(2,1)} %gather_fusion.5, bf16[4096,128]{1,0:T(8,128)(2,1)} %gather_fusion.4, bf16[4096,128]{1,0:T(8,128)(2,1)S(1)} %gather_fusion.3, ...), kind=kLoop, calls=%fused_computation.32 | loop fusion | flops 12582912 | bytes 9469952 | tf_op jit(solution)/shard_map/stack | solution.py:40
  133.6 2.7 reduce.6
  137.4 9.6 %all-to-all-start = ((bf16[64,2,4096]{2,1,0:T(2,128)(2,1)}), bf16[64,2,4096]{2,1,0:T(2,128)(2,1)}, u32[]{:S(2)}, u32[]{:S(2)}) async-start(bf16[64,2,4096]{2,1,0:T(2,128)(2,1)} %reshape.127), calls=%async_computation | async-start | bytes 2097152 | tf_op jit(solution)/shard_map/all_to_all | solution.py:41
  147.0 17.1 %all-to-all-done = bf16[64,2,4096]{2,1,0:T(2,128)(2,1)} async-done(((bf16[64,2,4096]{2,1,0:T(2,128)(2,1)}), bf16[64,2,4096]{2,1,0:T(2,128)(2,1)}, u32[]{:S(2)}, u32[]{:S(2)}) %all-to-all-start) | async-done | bytes 1048608 | tf_op jit(solution)/shard_map/all_to_all | solution.py:41
  164.1 6.5 %reshape.128 = bf16[4096,1,128]{2,1,0:T(2,128)(2,1)S(1)} reshape(bf16[64,2,4096]{2,1,0:T(2,128)(2,1)} %all-to-all-done) | data formatting | bytes 2097152
  171.7 2.0 gather_fusion
  173.9 34.6 %all_to_all.43 = bf16[64,64,128]{2,0,1:T(8,128)(2,1)S(1)} all-to-all(bf16[64,64,128]{2,0,1:T(8,128)(2,1)S(1)} %select_bitcast_fusion), channel_id=1, replica_groups=mesh['dp'=64,'mp'=4] {'mp'}, dimensions={1} | all-to-all | bytes 2097152 | tf_op jit(solution)/shard_map/all_to_all | solution.py:43
  211.0 3.5 all-to-all-start.2
  214.6 24.8 %all-to-all-done.2 = bf16[4,256,512]{2,1,0:T(8,128)(2,1)S(1)} async-done(((bf16[4,256,512]{2,1,0:T(8,128)(2,1)}), bf16[4,256,512]{2,1,0:T(8,128)(2,1)S(1)}, u32[]{:S(2)}, u32[]{:S(2)}) %all-to-all-start.2) | async-done | bytes 1048608 | tf_op jit(solution)/shard_map/all_to_all | solution.py:9
  239.6 2.6 fusion.2
  243.5 28.2 %all_to_all.44 = bf16[4,256,512]{2,1,0:T(8,128)(2,1)S(1)} all-to-all(bf16[4,256,512]{2,1,0:T(8,128)(2,1)S(1)} %broadcast_in_dim.38), channel_id=1, replica_groups=mesh['dp'=64,'mp'=4] {'mp'}, dimensions={0} | all-to-all | bytes 2097152 | tf_op jit(solution)/shard_map/all_to_all | solution.py:9
  272.0 3.8 fusion.3
  276.6 68.6 %all-gather.3.cloned.1.call-done = bf16[256,8192]{1,0:T(8,128)(2,1)} async-done(((bf16[256,2048]{1,0:T(8,128)(2,1)}), bf16[256,8192]{1,0:T(8,128)(2,1)}) %all-gather.3.cloned.1.call-update) | async-done | bytes 4194320 | tf_op jit(solution)/shard_map/all_gather | solution.py:67
  345.2 125.9 %all-gather.5.cloned.1.call-done = bf16[8192,512]{1,0:T(8,128)(2,1)} async-done(((bf16[128,512]{1,0:T(8,128)(2,1)}), bf16[8192,512]{1,0:T(8,128)(2,1)}) %all-gather.5.cloned.1.call-update) | async-done | bytes 8388624 | tf_op jit(solution)/shard_map/all_gather | solution.py:70
  471.1 7.7 %fusion.15 = bf16[256,512]{1,0:T(8,128)(2,1)} fusion(bf16[256,8192]{1,0:T(8,128)(2,1)} %all-gather.3.cloned.1.call-done, bf16[8192,512]{1,0:T(8,128)(2,1)} %all-gather.5.cloned.1.call-done, f32[512]{0:T(512)S(1)} %copy-done.4), kind=kOutput, calls=%fused_computation.29 | convolution fusion | flops 2147876864 | bytes 12847104 | tf_op jit(solution)/shard_map/dot_general | solution.py:68
  (48 shorter events, 9.1 us)
Async XLA Ops:
  6.5 3.0 copy-start
  136.2 10.7 %copy-start.5 = (s32[64]{0:T(128)S(1)}, s32[64]{0:T(128)}, u32[]{:S(2)}) copy-start(s32[64]{0:T(128)} %param.12) | copy-start | bytes 772
  137.4 26.7 %all-to-all-start = ((bf16[64,2,4096]{2,1,0:T(2,128)(2,1)}), bf16[64,2,4096]{2,1,0:T(2,128)(2,1)}, u32[]{:S(2)}, u32[]{:S(2)}) async-start(bf16[64,2,4096]{2,1,0:T(2,128)(2,1)} %reshape.127), calls=%async_computation | async-start | bytes 2097152 | tf_op jit(solution)/shard_map/all_to_all | solution.py:41
  173.9 35.3 %copy-start.2 = (bf16[2,2048,512]{2,1,0:T(8,128)(2,1)S(1)}, bf16[2,2048,512]{2,1,0:T(8,128)(2,1)}, u32[]{:S(2)}) copy-start(bf16[2,2048,512]{2,1,0:T(8,128)(2,1)} %param.13) | copy-start | bytes 12582916
  209.9 4.6 copy-start.1
  211.0 28.4 %all-to-all-start.2 = ((bf16[4,256,512]{2,1,0:T(8,128)(2,1)}), bf16[4,256,512]{2,1,0:T(8,128)(2,1)S(1)}, u32[]{:S(2)}, u32[]{:S(2)}) async-start(bf16[4,256,512]{2,1,0:T(8,128)(2,1)} %broadcast_in_dim.37), calls=%async_computation.2 | async-start | bytes 2097152 | tf_op jit(solution)/shard_map/all_to_all | solution.py:9
  214.5 130.7 %all-gather.3.cloned.1.call-start = ((), (), s32[]{:S(2)}) async-start(), calls=%async_computation.4 | async-start | bytes 5242880 | tf_op jit(solution)/shard_map/all_gather | solution.py:67
  239.6 2.8 copy-start.3
  242.5 1.0 copy-start.6
  272.0 199.1 %copy-start.4 = (f32[512]{0:T(512)S(1)}, f32[512]{0:T(512)}, u32[]{:S(2)}) copy-start(f32[512]{0:T(512)} %param.17) | copy-start | bytes 6148
  275.8 195.3 %all-gather.5.cloned.1.call-start = ((), (), s32[]{:S(2)}) async-start(), calls=%async_computation.5 | async-start | bytes 8519680 | tf_op jit(solution)/shard_map/all_gather | solution.py:70
Sparse Core Ops, SparseCore 0:
  275.9 69.2 all-gather.2
  347.0 124.0 all-gather.4
where the time goes:
time: 488 us; the launch traced here: 486 us
  waiting for transfers between devices  237 us (49%)
  local copies, waits for them, and re-layouts  130 us (27%)
  blocking collectives  62.9 us (13%)
  matrix products  15.5 us (3%)
  between operations  13.7 us (3%)
  other arithmetic  13.3 us (3%)
  starting transfers between devices  13.2 us (3%)
    all_gather x1, waiting for transfers between devices, body(): lax.all_gather(tower_weight, 'dp', axis=0, tiled=True)  126 us
    gather x8, local copies, waits for them, and re-layouts, body(): jnp.take(tables[0], own_ids[:, hot_index], axis=0).astype(jnp.float32)  114 us
    all_gather x1, waiting for transfers between devices, body(): full_rows = lax.all_gather(crossed, 'mp', axis=1, tiled=True)  68.6 us
    all_to_all x1, blocking collectives, body(): lax.all_to_all(ordered, 'mp', split_axis=1, concat_axis=0, tiled=True)  34.6 us
    all_to_all x1, blocking collectives, from_everyone(): lax.all_to_all(jnp.broadcast_to(x[None], (length, *x.shape)), axis, 0, 0,...  28.2 us
    all_to_all x1, waiting for transfers between devices, from_everyone(): lax.all_to_all(jnp.broadcast_to(x[None], (length, *x.shape)), axis, 0, 0,...  24.8 us
    all_to_all x1, waiting for transfers between devices, body(): lax.all_to_all(pooled, 'dp', split_axis=0, concat_axis=1, tiled=True)  17.1 us
    another operation x2, other arithmetic, body(): pooled = jnp.stack(columns, axis=1)  12.5 us
  transfers between devices with their start and end apart: 4, of which 4 were waited for; matrix products, arithmetic and copies ran while one was open for 0% of the time, Pallas kernels for 0%

commit v1 on v0

v1 whole, which is shorter than its diff:
```python
import functools

import jax
import jax.numpy as jnp
from jax import lax
from jax.experimental import pallas as pl
from jax.experimental.pallas import tpu as pltpu
from jax.sharding import PartitionSpec as P

MESH = pl.DeviceIdType.MESH
VMEM = pltpu.VMEM
F32 = jnp.float32
BF16 = jnp.bfloat16
WHOLE = pl.BlockSpec(memory_space=pltpu.VMEM)
SCALARS = pl.BlockSpec(memory_space=pltpu.SMEM)


def pool_kernel(hots, blocks, rows, ids_ref, table_ref, out_ref, wide, acc):
    vocab = table_ref.shape[0]
    samples = blocks * rows
    step = 256

    def widen(i, carry):
        at = pl.ds(pl.multiple_of(i * step, step), step)
        wide[at, :] = table_ref[at, :].astype(F32)
        return carry

    lax.fori_loop(0, vocab // step, widen, 0)

    def block(g, carry):
        def eight(q, carry):
            first = g * rows + q * 8
            for j in range(8):
                total = wide[pl.ds(ids_ref[first + j], 1), :]
                for h in range(1, hots):
                    total = total + wide[pl.ds(ids_ref[h * samples + first + j], 1), :]
                acc[pl.ds(q * 8 + j, 1), :] = total
            return carry

        lax.fori_loop(0, rows // 8, eight, 0)
        out_ref[g] = acc[...].astype(BF16)
        return carry

    lax.fori_loop(0, blocks, block, 0)


def pooled_rows(own_ids, table, hots, blocks, rows):
    vocab, width = table.shape
    return pl.pallas_call(
        functools.partial(pool_kernel, hots, blocks, rows),
        out_shape=jax.ShapeDtypeStruct((blocks, rows, width), BF16),
        in_specs=[SCALARS, WHOLE],
        out_specs=WHOLE,
        scratch_shapes=[VMEM((vocab, width), F32), VMEM((rows, width), F32)],
        name="pool",
        cost_estimate=pl.CostEstimate(flops=40_000_000_000, bytes_accessed=3_000_000, transcendentals=0),
    )(own_ids, table)


def barrier_with(others):
    barrier = pltpu.get_barrier_semaphore()
    count = 0
    for loop, device in others:
        def one(k, carry, device=device):
            pl.semaphore_signal(barrier, inc=1, device_id=device(k), device_id_type=MESH)
            return carry

        lax.fori_loop(1, loop, one, 0)
        count += loop - 1
    pl.semaphore_wait(barrier, count)


def regroup_kernel(groups, members, order_ref, pooled_ref, emb_ref, recv, packed, send_sem, recv_sem, mp_send, mp_recv):
    d = lax.axis_index("dp")
    m = lax.axis_index("mp")
    rows, width = pooled_ref.shape[1:]
    per = groups // members

    def dp_at(k):
        return (lax.rem(d + k, groups), m)

    def mp_at(k):
        return (d, lax.rem(m + k, members))

    barrier_with(((groups, dp_at), (members, mp_at)))

    def dp_copy(k):
        return pltpu.make_async_remote_copy(
            src_ref=pooled_ref.at[lax.rem(d + k, groups)],
            dst_ref=recv.at[d],
            send_sem=send_sem,
            recv_sem=recv_sem,
            device_id=dp_at(k),
            device_id_type=MESH,
        )

    def start(k, carry):
        dp_copy(k).start()
        return carry

    lax.fori_loop(1, groups, start, 0)
    recv[d] = pooled_ref[d]
    every = pltpu.make_async_remote_copy(
        src_ref=pooled_ref.at[pl.ds(0, groups - 1)],
        dst_ref=recv.at[pl.ds(0, groups - 1)],
        send_sem=send_sem,
        recv_sem=recv_sem,
        device_id=dp_at(1),
        device_id_type=MESH,
    )
    every.wait_recv()
    for p in range(groups):
        packed[p // per, :, (p % per) * width : (p % per + 1) * width] = recv[order_ref[p]]
    copies = []
    for k in range(1, members):
        to = lax.rem(m + k, members)
        copies.append(
            pltpu.make_async_remote_copy(
                src_ref=packed.at[to],
                dst_ref=emb_ref.at[m],
                send_sem=mp_send.at[k - 1],
                recv_sem=mp_recv.at[k - 1],
                device_id=mp_at(k),
                device_id_type=MESH,
            )
        )
        copies[-1].start()
    emb_ref[m] = packed[m]
    every.wait_send()
    for copy in copies:
        copy.wait()


def regrouped(pooled, order, groups, members):
    _, rows, width = pooled.shape
    per = groups // members
    return pl.pallas_call(
        functools.partial(regroup_kernel, groups, members),
        out_shape=jax.ShapeDtypeStruct((members, rows, per * width), BF16),
        in_specs=[SCALARS, WHOLE],
        out_specs=WHOLE,
        scratch_shapes=[
            VMEM((groups, rows, width), BF16),
            VMEM((members, rows, per * width), BF16),
            pltpu.SemaphoreType.DMA,
            pltpu.SemaphoreType.DMA,
            pltpu.SemaphoreType.DMA((members - 1,)),
            pltpu.SemaphoreType.DMA((members - 1,)),
        ],
        compiler_params=pltpu.CompilerParams(collective_id=0, has_side_effects=True),
        name="regroup",
        cost_estimate=pl.CostEstimate(flops=40_000_000_000, bytes_accessed=3_000_000, transcendentals=0),
    )(order, pooled)


def cross_kernel(
    members, emb_ref, down_ref, up_ref, bias_ref, tower_ref, tower_bias_ref, out_ref,
    part, arrived, proj, crossed, partial_units, units_in, send_sem, recv_sem,
):
    d = lax.axis_index("dp")
    m = lax.axis_index("mp")
    rows, cols = emb_ref.shape
    layers, _, rank = down_ref.shape
    share = rows // members
    units = out_ref.shape[1]

    def mp_at(k):
        return (d, lax.rem(m + k, members))

    barrier_with(((members, mp_at),))

    def copy_to(k, phase, src, dst):
        return pltpu.make_async_remote_copy(
            src_ref=src,
            dst_ref=dst,
            send_sem=send_sem.at[phase, k - 1],
            recv_sem=recv_sem.at[phase, k - 1],
            device_id=mp_at(k),
            device_id_type=MESH,
        )

    tile = min(512, cols)
    for layer in range(layers):
        source = emb_ref if layer == 0 else crossed
        product = jnp.dot(source[...], down_ref[layer], preferred_element_type=F32)
        part[layer] = product.astype(BF16).reshape(members, share, rank)
        copies = []
        for k in range(1, members):
            to = lax.rem(m + k, members)
            copies.append(copy_to(k, 2 * layer, part.at[layer, to], arrived.at[layer, k - 1]))
            copies[-1].start()
        total = part[layer, m].astype(F32)
        for k in range(1, members):
            copies[k - 1].wait()
            total = total + arrived[layer, k - 1].astype(F32)
        proj[layer, m] = total.astype(BF16)
        copies = []
        for k in range(1, members):
            copies.append(copy_to(k, 2 * layer + 1, proj.at[layer, m], proj.at[layer, m]))
            copies[-1].start()
        for copy in copies:
            copy.wait()
        projected = proj[layer].reshape(rows, rank)

        def columns(i, carry, layer=layer, source=source, projected=projected):
            at = pl.ds(pl.multiple_of(i * tile, tile), tile)
            lifted = lax.dot_general(
                projected, up_ref[layer, at, :], (((1,), (1,)), ((), ())), preferred_element_type=F32
            )
            value = emb_ref[:, at].astype(F32) * (lifted + bias_ref[layer : layer + 1, at])
            crossed[:, at] = (value + source[:, at].astype(F32)).astype(BF16)
            return carry

        lax.fori_loop(0, cols // tile, columns, 0)

    def tower(block):
        at = pl.ds(pl.multiple_of(block * cols, cols), cols)
        return jnp.dot(crossed[...], tower_ref[at, :], preferred_element_type=F32)

    def send_units(k, carry):
        to = lax.rem(m + k, members)
        partial_units[k - 1] = tower(to).astype(BF16)
        copy_to(k, 2 * layers, partial_units.at[k - 1], units_in.at[k - 1]).start()
        return carry

    lax.fori_loop(1, members, send_units, 0)
    total = tower(m) + tower_bias_ref[...]
    for k in range(1, members):
        copy_to(k, 2 * layers, partial_units.at[k - 1], units_in.at[k - 1]).wait()
        total = total + units_in[k - 1].astype(F32)
    out_ref[...] = jnp.maximum(total, 0.0).astype(BF16)


def crossed_and_towered(emb, down, up, bias, tower, tower_bias, members):
    rows, cols = emb.shape
    layers, _, rank = down.shape
    units = tower.shape[1]
    share = rows // members
    phases = 2 * layers + 1
    return pl.pallas_call(
        functools.partial(cross_kernel, members),
        out_shape=jax.ShapeDtypeStruct((rows, units), BF16),
        in_specs=[WHOLE] * 6,
        out_specs=WHOLE,
        scratch_shapes=[
            VMEM((layers, members, share, rank), BF16),
            VMEM((layers, members - 1, share, rank), BF16),
            VMEM((layers, members, share, rank), BF16),
            VMEM((rows, cols), BF16),
            VMEM((members - 1, rows, units), BF16),
            VMEM((members - 1, rows, units), BF16),
            pltpu.SemaphoreType.DMA((phases, members - 1)),
            pltpu.SemaphoreType.DMA((phases, members - 1)),
        ],
        compiler_params=pltpu.CompilerParams(
            collective_id=1, has_side_effects=True, vmem_limit_bytes=48 * 1024 * 1024
        ),
        name="cross",
        cost_estimate=pl.CostEstimate(flops=4_000_000_000, bytes_accessed=20_000_000, transcendentals=0),
    )(emb, down, up, bias, tower, tower_bias)


def body(groups, members, feature_ids, tables, table_of_feature, cross_down, cross_up, cross_bias, tower_weight, tower_bias):
    m = lax.axis_index("mp")
    _, batch, hots = feature_ids.shape
    rows = batch // (groups * members)
    per = groups // members
    swap = []
    for a in range(members):
        for b in range(per):
            for z in range(members):
                swap.append(((a * per + b) * members + z, (z * per + b) * members + a))
    turned = lax.ppermute(tower_weight, ("dp", "mp"), swap)
    tower = lax.all_gather(turned, "dp", axis=0, tiled=True)
    by_hot = jnp.transpose(feature_ids[0]).reshape(hots, groups, members, rows)
    own_ids = lax.dynamic_index_in_dim(by_hot, m, 2, keepdims=False).reshape(-1)
    pooled = pooled_rows(own_ids, tables[0], hots, groups, rows)
    emb = regrouped(pooled, table_of_feature, groups, members)
    emb = emb.reshape(members * rows, -1)
    return crossed_and_towered(
        emb, cross_down, cross_up, cross_bias, tower, tower_bias.reshape(1, -1), members
    )


def solution(mesh):
    groups, members = mesh.shape["dp"], mesh.shape["mp"]
    return jax.shard_map(
        functools.partial(body, groups, members),
        mesh=mesh,
        in_specs=(
            P("dp", None, None),
            P("dp", None, None),
            P(),
            P(None, "mp", None),
            P(None, "mp", None),
            P(None, "mp"),
            P("dp", "mp"),
            P("mp"),
        ),
        out_specs=P("dp", "mp"),
        check_vma=False,
    )
```

time: 488 us -> 248 us (0.51)
  waiting for transfers between devices: 237 us -> 44.1 us
  Pallas kernels: 0 us -> 181 us
  local copies, waits for them, and re-layouts: 130 us -> 8.05 us
  blocking collectives: 62.9 us -> 0 us
  matrix products: 15.5 us -> 0 us
  other arithmetic: 13.3 us -> 0 us
  starting transfers between devices: 13.2 us -> 1.55 us
    pallas_call x0 -> x3, Pallas kernels: none -> 181 us  [the longest x1 80.2 us: crossed_and_towered(): pl.pallas_call(functools.partial(cross_kernel, members), out_shape=jax.Sh...]
    all_gather x2 -> x1, waiting for transfers between devices: 195 us -> 44.1 us  [body(): tower = lax.all_gather(turned, 'dp', axis=0, tiled=True)]
    gather x9 -> x0, local copies, waits for them, and re-layouts: 116 us -> none  [the longest x8 114 us: body(): jnp.take(tables[0], own_ids[:, hot_index], axis=0).astype(jnp.float32)]
    all_to_all x2 -> x0, blocking collectives: 62.9 us -> none  [the longest x1 34.6 us: body(): lax.all_to_all(ordered, 'mp', split_axis=1, concat_axis=0, tiled=True)]
    all_to_all x2 -> x0, waiting for transfers between devices: 41.9 us -> none  [the longest x1 24.8 us: from_everyone(): lax.all_to_all(jnp.broadcast_to(x[None], (length, *x.shape)), axis, 0, 0,...]
    dot_general x5 -> x0, matrix products: 15.5 us -> none  [the longest x1 7.69 us: body(): jnp.dot(full_rows, lax.all_gather(tower_weight, 'dp', axis=0, tiled=True)...]
    all_to_all x2 -> x0, starting transfers between devices: 13.1 us -> none  [the longest x1 9.56 us: body(): lax.all_to_all(pooled, 'dp', split_axis=0, concat_axis=1, tiled=True)]
    another operation x2 -> x0, other arithmetic: 12.5 us -> none  [body(): pooled = jnp.stack(columns, axis=1)]
  transfers between devices with their start and end apart: 4 -> 2, of which waited for: 4 -> 1; matrix products, arithmetic and copies ran while one was open for 0% -> 1% of each run, Pallas kernels for 0% -> 41%
where the time goes in v1:
time: 248 us
  Pallas kernels  181 us (73%)
  waiting for transfers between devices  44.1 us (18%)
  between operations  13.4 us (5%)
  local copies, waits for them, and re-layouts  8.05 us (3%)
    pallas_call x1, Pallas kernels, crossed_and_towered(): pl.pallas_call(functools.partial(cross_kernel, members), out_shape=jax.Sh...  80.2 us
    pallas_call x1, Pallas kernels, regrouped(): pl.pallas_call(functools.partial(regroup_kernel, groups, members), out_sh...  66.5 us
    all_gather x1, waiting for transfers between devices, body(): tower = lax.all_gather(turned, 'dp', axis=0, tiled=True)  44.1 us
    pallas_call x1, Pallas kernels, pooled_rows(): pl.pallas_call(functools.partial(pool_kernel, hots, blocks, rows), out_sh...  34.2 us
  transfers between devices with their start and end apart: 2, of which 1 were waited for; matrix products, arithmetic and copies ran while one was open for 1% of the time, Pallas kernels for 41%

profile of v1, /device:TPU:2, one launch (start us, length us, event | category | flops | bytes accessed | tf_op | source)
XLA Modules:
  0.0 248.1 jit_solution(11946547683913608700)
XLA Ops:
  6.5 0.0 all-gather.2.cloned.1.call-start
  6.5 1.6 collective-permute-start
  8.1 0.0 collective-permute-done
  8.1 0.0 copy-start.4
  8.1 0.7 copy-done.4
  8.7 0.0 all-gather.2.cloned.1.call-update
  8.8 1.7 reshape.13
  10.5 0.8 dynamic-slice_reduce_fusion
  11.3 0.8 reshape.14.ids_ref
  12.1 34.2 %pool.1.pooled_ref = bf16[64,64,128]{2,1,0:T(8,128)(2,1)} custom-call(s32[32768]{0:T(1024)} %reshape.14.ids_ref, bf16[4096,128]{1,0:T(8,128)(2,1)} %bitcast.9), custom_call_target="tpu_custom_call" | custom-call | flops 40000000000 | bytes 3000000 | tf_op jit(solution)/shard_map/pool/pallas_call | solution.py:49
  46.3 0.0 copy-start.2
  46.3 0.0 copy-start.3
  46.3 66.5 %regroup.1 = bf16[4,64,2048]{2,1,0:T(8,128)(2,1)} custom-call(s32[64]{0:T(128)} %order_ref.1, bf16[64,64,128]{2,1,0:T(8,128)(2,1)} %pool.1.pooled_ref), custom_call_target="tpu_custom_call" | custom-call | flops 40000000000 | bytes 3000000 | tf_op jit(solution)/shard_map/regroup/pallas_call | solution.py:137
  112.8 44.1 %all-gather.2.cloned.1.call-done.tower_ref = bf16[8192,512]{1,0:T(8,128)(2,1)} async-done(((bf16[128,512]{1,0:T(8,128)(2,1)}), bf16[8192,512]{1,0:T(8,128)(2,1)}) %all-gather.2.cloned.1.call-update) | async-done | bytes 8388624 | tf_op jit(solution)/shard_map/all_gather | solution.py:274
  156.9 0.0 copy-done.2
  156.9 0.0 copy-done.3
  156.9 0.0 copy-start
  156.9 2.2 copy-done
  159.1 0.0 copy-start.1
  159.1 1.2 copy-done.1
  160.3 80.2 %cross.1 = bf16[256,512]{1,0:T(8,128)(2,1)S(1)} custom-call(bf16[256,2048]{1,0:T(8,128)(2,1)S(1)} %bitcast.6, bf16[2,2048,512]{2,1,0:T(8,128)(2,1)S(1)} %copy-done, bf16[2,2048,512]{2,1,0:T(8,128)(2,1)} %up_ref.1, f32[2,2048]{1,0:T(2,128)S(1)} %copy-done.2, bf16[8192,512]{1,0:T(8,128)(2,1)} %all-gather.2.cloned.1.call-done.tower_ref, f32[1,512]{1,0:T(1,128)S(1)} %bitcast.7), custom_call_target="tpu_custom_call" | custom-call | flops 4000000000 | bytes 20000000 | tf_op jit(solution)/shard_map/cross/pallas_call | solution.py:240
  240.5 0.7 copy.10
Async XLA Ops:
  6.5 150.4 %all-gather.2.cloned.1.call-start = ((), (), s32[]{:S(2)}) async-start(), calls=%async_computation | async-start | bytes 8519680 | tf_op jit(solution)/shard_map/all_gather | solution.py:274
  6.5 1.6 collective-permute-start
  8.1 0.7 copy-start.4
  46.3 110.6 %copy-start.2 = (f32[2,2048]{1,0:T(2,128)S(1)}, f32[2,2048]{1,0:T(2,128)}, u32[]{:S(2)}) copy-start(f32[2,2048]{1,0:T(2,128)} %bias_ref.1) | copy-start | bytes 49156
  46.3 110.6 %copy-start.3 = (f32[512]{0:T(512)S(1)}, f32[512]{0:T(512)}, u32[]{:S(2)}) copy-start(f32[512]{0:T(512)} %param.15) | copy-start | bytes 6148
  156.9 2.2 copy-start
  159.1 1.2 copy-start.1
Sparse Core Ops, SparseCore 0:
  9.2 147.6 all-gather.1

commit v2 on v0

v2 whole, which is shorter than its diff:
```python
import functools

import jax
import jax.numpy as jnp
from jax import lax
from jax.experimental import pallas as pl
from jax.experimental.pallas import tpu as pltpu
from jax.sharding import PartitionSpec as P

MESH = pl.DeviceIdType.MESH
VMEM = pltpu.VMEM
DMA = pltpu.SemaphoreType.DMA
F32 = jnp.float32
BF16 = jnp.bfloat16
WHOLE = pl.BlockSpec(memory_space=pltpu.VMEM)
SCALARS = pl.BlockSpec(memory_space=pltpu.SMEM)
ANY = pl.BlockSpec(memory_space=pl.ANY)
LANES = 128
CHUNKS = 4
GROUPS = 2


def torus(groups, members):
    rest = groups // members
    across = min(4, rest)
    rest //= across
    below = min(2, rest)
    return members, across, below, rest // below


def place(sizes, d):
    _, nx, nz, nc = sizes
    return d // (nx * nz * nc), lax.rem(d // (nz * nc), nx), lax.rem(d // nc, nz), lax.rem(d, nc)


def index_of(sizes, y, x, z, c):
    _, nx, nz, nc = sizes
    return ((y * nx + x) * nz + z) * nc + c


def signal(device):
    pl.semaphore_signal(pltpu.get_barrier_semaphore(), inc=1, device_id=device, device_id_type=MESH)


def remote(src, dst, send, recv, device):
    return pltpu.make_async_remote_copy(
        src_ref=src, dst_ref=dst, send_sem=send, recv_sem=recv, device_id=device, device_id_type=MESH
    )


def regroup_kernel(
    groups, members, hots, ids_hbm, order_ref, table_ref, weight_ref, emb_ref, quarter_ref,
    ids_ref, wide, acc, pooled, recv, packed, mine, ids_sem,
    send_sem, recv_sem, mp_send, mp_recv, w_send, w_recv,
):
    d = lax.axis_index("dp")
    m = lax.axis_index("mp")
    vocab, width = table_ref.shape
    chunk = pooled.shape[2]
    per = groups // members
    sizes = torus(groups, members)
    ny, nx, nz, nc = sizes
    y, x, z, c = place(sizes, d)

    ids_copy = pltpu.make_async_copy(ids_hbm, ids_ref, ids_sem)
    ids_copy.start()

    def dp_at(k):
        return (lax.rem(d + k, groups), m)

    def mp_at(k):
        return (d, lax.rem(m + k, members))

    turned = (m * per + lax.rem(d, per), d // per)
    moved = d // per != m
    for count, device in ((groups, dp_at), (members, mp_at)):

        def greet(k, carry, device=device):
            signal(device(k))
            return carry

        lax.fori_loop(1, count, greet, 0)

    @pl.when(moved)
    def _():
        signal(turned)

    pl.semaphore_wait(
        pltpu.get_barrier_semaphore(), groups + members - 2 + jnp.where(moved, 1, 0).astype(jnp.int32)
    )

    swap = remote(weight_ref, mine, w_send.at[0], w_recv.at[0], turned)

    @pl.when(moved)
    def _():
        swap.start()

    @pl.when(jnp.logical_not(moved))
    def _():
        mine[...] = weight_ref[...]

    step = 256

    def widen(i, carry):
        at = pl.ds(pl.multiple_of(i * step, step), step)
        wide[at, :] = table_ref[at, :].astype(F32)
        return carry

    lax.fori_loop(0, vocab // step, widen, 0)
    ids_copy.wait()

    rows = CHUNKS * chunk
    parts_in_tile = LANES // rows if rows < LANES else 1
    lane0 = lax.rem(m, parts_in_tile) * rows
    span = hots * LANES

    def lookups(ch, g):
        near = ids_ref.at[pl.ds(g * span + lane0 + ch * chunk, (hots - 1) * LANES + chunk)]
        for j in range(chunk):
            total = wide[pl.ds(near[j], 1), :]
            for h in range(1, hots):
                total = total + wide[pl.ds(near[h * LANES + j], 1), :]
            acc[j : j + 1, :] = total

    def dp_copy(ch, k):
        return remote(
            pooled.at[ch, lax.rem(d + k, groups)], recv[ch].at[d], send_sem.at[ch], recv_sem.at[ch], dp_at(k)
        )

    def every(ch):
        some = pl.ds(0, groups - 1)
        return remote(pooled.at[ch, some], recv[ch].at[some], send_sem.at[ch], recv_sem.at[ch], dp_at(1))

    def pool(ch):
        lookups(ch, lax.rem(d + 1, groups))

        def block(k, carry):
            pooled[ch, lax.rem(d + k - 1, groups)] = acc[...].astype(BF16)
            lookups(ch, lax.rem(d + k, groups))
            dp_copy(ch, k - 1).start()
            return carry

        lax.fori_loop(2, groups, block, 0)
        pooled[ch, lax.rem(d + groups - 1, groups)] = acc[...].astype(BF16)
        lookups(ch, d)
        dp_copy(ch, groups - 1).start()
        recv[ch][d] = acc[...].astype(BF16)

    def mp_copy(ch, k):
        to = lax.rem(m + k, members)
        at = pl.ds(ch * chunk, chunk)
        return remote(packed.at[ch, to], emb_ref.at[m, at], mp_send.at[ch, k - 1], mp_recv.at[ch, k - 1], mp_at(k))

    def spread(ch):
        every(ch).wait_recv()
        for p in range(groups):
            packed[ch, p // per, :, (p % per) * width : (p % per + 1) * width] = recv[ch][order_ref[p]]
        emb_ref[m, ch * chunk : (ch + 1) * chunk, :] = packed[ch, m]
        for k in range(1, members):
            mp_copy(ch, k).start()

    def at_xyz(y, x, z):
        return (index_of(sizes, y, x, z, c), m)

    right, left = lax.rem(x + 1, nx), lax.rem(x + nx - 1, nx)
    upper, lower = lax.rem(y + 1, ny), lax.rem(y + ny - 1, ny)
    half = mine.shape[1] // 2
    first, second = pl.ds(0, half), pl.ds(half, half)

    def below():
        other = 1 - z
        return [
            remote(mine.at[0], quarter_ref.at[0, x, z], w_send.at[1], w_recv.at[1], at_xyz(y, x, other)),
            remote(mine.at[1], quarter_ref.at[1, y, z], w_send.at[2], w_recv.at[2], at_xyz(y, x, other)),
        ]

    def beside():
        copies = []
        if nx > 1:
            own = quarter_ref.at[0, x]
            copies.append(remote(own, own, w_send.at[3], w_recv.at[3], at_xyz(y, right, z)))
            copies.append(remote(own, own, w_send.at[4], w_recv.at[4], at_xyz(y, left, z)))
        own = quarter_ref.at[1, y]
        copies.append(remote(own, own, w_send.at[5], w_recv.at[5], at_xyz(upper, x, z)))
        copies.append(remote(own, own, w_send.at[6], w_recv.at[6], at_xyz(lower, x, z)))
        return copies

    def relayed():
        copies = []
        if nx > 1:
            part = quarter_ref.at[0, left, :, first]
            copies.append(remote(part, part, w_send.at[7], w_recv.at[7], at_xyz(y, right, z)))
            part = quarter_ref.at[0, right, :, second]
            copies.append(remote(part, part, w_send.at[8], w_recv.at[8], at_xyz(y, left, z)))
        part = quarter_ref.at[1, lower, :, first]
        copies.append(remote(part, part, w_send.at[9], w_recv.at[9], at_xyz(upper, x, z)))
        part = quarter_ref.at[1, upper, :, second]
        copies.append(remote(part, part, w_send.at[10], w_recv.at[10], at_xyz(lower, x, z)))
        return copies

    def start(copies):
        for copy in copies:
            copy.start()

    def wait(copies):
        for copy in copies:
            copy.wait()

    pool(0)

    @pl.when(moved)
    def _():
        swap.wait()

    if nz > 1:
        start(below())
    quarter_ref[0, x, z] = mine[0]
    quarter_ref[1, y, z] = mine[1]
    pool(1)
    spread(0)
    if nz > 1:
        wait(below())
    start(beside())
    pool(2)
    spread(1)
    wait(beside())
    start(relayed())
    pool(3)
    spread(2)
    spread(3)
    wait(relayed())
    for ch in range(CHUNKS):
        every(ch).wait_send()
        for k in range(1, members):
            mp_copy(ch, k).wait()


def regrouped(ids, order, table, weight, groups, members, hots, rows):
    vocab, width = table.shape
    per = groups // members
    chunk = rows // CHUNKS
    ny, nx, nz, _ = torus(groups, members)
    depth, units = weight.shape[1:]
    return pl.pallas_call(
        functools.partial(regroup_kernel, groups, members, hots),
        out_shape=[
            jax.ShapeDtypeStruct((members, rows, per * width), BF16),
            jax.ShapeDtypeStruct((2, max(ny, nx), nz, depth, units), BF16),
        ],
        in_specs=[ANY, SCALARS, WHOLE, WHOLE],
        out_specs=[WHOLE, WHOLE],
        scratch_shapes=[
            pltpu.SMEM(ids.shape, jnp.int32),
            VMEM((vocab, width), F32),
            VMEM((chunk, width), F32),
            VMEM((CHUNKS, groups, chunk, width), BF16),
            [VMEM((groups, chunk, width), BF16) for _ in range(CHUNKS)],
            VMEM((CHUNKS, members, chunk, per * width), BF16),
            VMEM((2, depth, units), BF16),
            DMA,
            DMA((CHUNKS,)),
            DMA((CHUNKS,)),
            DMA((CHUNKS, members - 1)),
            DMA((CHUNKS, members - 1)),
            DMA((11,)),
            DMA((11,)),
        ],
        compiler_params=pltpu.CompilerParams(collective_id=0, has_side_effects=True),
        name="regroup",
    )(ids, order, table, weight)


def cross_kernel(
    groups, members, emb_ref, quarter_ref, down_hbm, up_hbm, bias_ref, tower_bias_ref, out_ref,
    down_ref, up_ref, tower_ref, part, arrived, proj, crossed, sums, partial_units, units_in,
    load_sem, send_sem, recv_sem, w_send, w_recv,
):
    d = lax.axis_index("dp")
    m = lax.axis_index("mp")
    rows, cols = emb_ref.shape
    layers, _, rank = down_ref.shape
    height = rows // GROUPS
    share = height // members
    units = out_ref.shape[1]
    sizes = torus(groups, members)
    ny, nx, nz, nc = sizes
    y, x, z, c = place(sizes, d)

    loads = []
    for layer in range(layers):
        loads.append(pltpu.make_async_copy(down_hbm.at[layer], down_ref.at[layer], load_sem.at[2 * layer]))
        loads.append(pltpu.make_async_copy(up_hbm.at[layer], up_ref.at[layer], load_sem.at[2 * layer + 1]))
    loads.append(pltpu.make_async_copy(
        quarter_ref.at[0, pl.ds(0, nx)], tower_ref.at[y, :, :, c, 0], load_sem.at[2 * layers]
    ))
    loads.append(pltpu.make_async_copy(
        quarter_ref.at[1, pl.ds(0, ny)], tower_ref.at[:, x, :, c, 1], load_sem.at[2 * layers + 1]
    ))
    for load in loads:
        load.start()

    def mp_at(k):
        return (d, lax.rem(m + k, members))

    def at_xyc(y, x, c):
        return (index_of(sizes, y, x, z, c), m)

    right, left = lax.rem(x + 1, nx), lax.rem(x + nx - 1, nx)
    upper, lower = lax.rem(y + 1, ny), lax.rem(y + ny - 1, ny)
    near = [mp_at(k) for k in range(1, members)]
    near += [at_xyc(upper, x, c), at_xyc(lower, x, c)]
    if nx > 1:
        near += [at_xyc(y, right, c), at_xyc(y, left, c)]
    if nc > 1:
        near.append(at_xyc(y, x, 1 - c))
    for device in near:
        signal(device)
    pl.semaphore_wait(pltpu.get_barrier_semaphore(), len(near))

    def first_way():
        to = tower_ref.at[y, :, :, c, 0]
        src = quarter_ref.at[0, pl.ds(0, nx)]
        copies = [
            remote(src, to, w_send.at[0], w_recv.at[0], at_xyc(upper, x, c)),
            remote(src, to, w_send.at[1], w_recv.at[1], at_xyc(lower, x, c)),
        ]
        if nx > 1:
            to = tower_ref.at[:, x, :, c, 1]
            src = quarter_ref.at[1, pl.ds(0, ny)]
            copies.append(remote(src, to, w_send.at[2], w_recv.at[2], at_xyc(y, right, c)))
            copies.append(remote(src, to, w_send.at[3], w_recv.at[3], at_xyc(y, left, c)))
        return copies

    depth = quarter_ref.shape[3]
    first, second = pl.ds(0, depth // 2), pl.ds(depth // 2, depth // 2)

    def second_way():
        part = tower_ref.at[lower, :, :, c, 0, first]
        copies = [remote(part, part, w_send.at[4], w_recv.at[4], at_xyc(upper, x, c))]
        part = tower_ref.at[upper, :, :, c, 0, second]
        copies.append(remote(part, part, w_send.at[5], w_recv.at[5], at_xyc(lower, x, c)))
        if nx > 1:
            part = tower_ref.at[:, left, :, c, 1, first]
            copies.append(remote(part, part, w_send.at[6], w_recv.at[6], at_xyc(y, right, c)))
            part = tower_ref.at[:, right, :, c, 1, second]
            copies.append(remote(part, part, w_send.at[7], w_recv.at[7], at_xyc(y, left, c)))
        return copies

    def pair():
        if nc == 1:
            return []
        part = tower_ref.at[:, :, :, c]
        return [remote(part, part, w_send.at[8], w_recv.at[8], at_xyc(y, x, 1 - c))]

    def start(copies):
        for copy in copies:
            copy.start()

    def wait(copies):
        for copy in copies:
            copy.wait()

    def rows_of(g):
        return pl.ds(g * height, height)

    def scatter(layer, g):
        i = layer * GROUPS + g
        return [
            remote(
                part.at[i, lax.rem(m + k, members)],
                arrived.at[i, k - 1],
                send_sem.at[2 * i, k - 1],
                recv_sem.at[2 * i, k - 1],
                mp_at(k),
            )
            for k in range(1, members)
        ]

    def gather(layer, g):
        i = layer * GROUPS + g
        return [
            remote(
                proj.at[i, m], proj.at[i, m], send_sem.at[2 * i + 1, k - 1], recv_sem.at[2 * i + 1, k - 1], mp_at(k)
            )
            for k in range(1, members)
        ]

    def project(layer, g):
        source = emb_ref if layer == 0 else crossed
        product = jnp.dot(source[rows_of(g), :], down_ref[layer], preferred_element_type=F32)
        i = layer * GROUPS + g
        part[i] = product.astype(BF16).reshape(members, share, rank)
        start(scatter(layer, g))

    def add_up(layer, g):
        i = layer * GROUPS + g
        wait(scatter(layer, g))
        total = part[i, m].astype(F32)
        for k in range(1, members):
            total = total + arrived[i, k - 1].astype(F32)
        proj[i, m] = total.astype(BF16)
        start(gather(layer, g))

    tile = min(512, cols)

    def lift(layer, g):
        i = layer * GROUPS + g
        wait(gather(layer, g))
        source = emb_ref if layer == 0 else crossed
        projected = proj[i].reshape(height, rank)
        here = rows_of(g)

        def columns(j, carry):
            at = pl.ds(pl.multiple_of(j * tile, tile), tile)
            lifted = lax.dot_general(
                projected, up_ref[layer, at, :], (((1,), (1,)), ((), ())), preferred_element_type=F32
            )
            value = emb_ref[here, at].astype(F32) * (lifted + bias_ref[layer : layer + 1, at])
            crossed[here, at] = (value + source[here, at].astype(F32)).astype(BF16)
            return carry

        lax.fori_loop(0, cols // tile, columns, 0)

    def tower(g, block):
        weights = tower_ref[block].reshape(cols, units)
        return jnp.dot(crossed[rows_of(g), :], weights, preferred_element_type=F32)

    def exchange(g, k):
        i = 2 * layers * GROUPS + g
        return remote(
            partial_units.at[g, k - 1], units_in.at[g, k - 1], send_sem.at[i, k - 1], recv_sem.at[i, k - 1], mp_at(k)
        )

    start(first_way())
    loads[0].wait()
    for g in range(GROUPS):
        project(0, g)
    for g in range(GROUPS):
        add_up(0, g)
    wait(first_way())
    start(second_way())
    loads[1].wait()
    loads[2].wait()
    for layer in range(1, layers):
        for g in range(GROUPS):
            lift(layer - 1, g)
            project(layer, g)
        if layer == 1:
            wait(second_way())
            for load in loads[2 * layers :]:
                load.wait()
            start(pair())
        for g in range(GROUPS):
            add_up(layer, g)
    for load in loads[3 : 2 * layers]:
        load.wait()
    for g in range(GROUPS):
        lift(layers - 1, g)
        if g == 0:
            wait(pair())

        def send_units(k, carry, g=g):
            partial_units[g, k - 1] = tower(g, lax.rem(m + k, members)).astype(BF16)
            exchange(g, k).start()
            return carry

        lax.fori_loop(1, members, send_units, 0)
        sums[rows_of(g), :] = tower(g, m) + tower_bias_ref[...]
    for g in range(GROUPS):
        total = sums[rows_of(g), :]
        for k in range(1, members):
            exchange(g, k).wait()
            total = total + units_in[g, k - 1].astype(F32)
        out_ref[rows_of(g), :] = jnp.maximum(total, 0.0).astype(BF16)


def crossed_and_towered(emb, quarter, down, up, bias, tower_bias, groups, members):
    rows, cols = emb.shape
    layers, _, rank = down.shape
    depth, units = quarter.shape[3:]
    height = rows // GROUPS
    share = height // members
    steps = layers * GROUPS
    phases = 2 * steps + GROUPS
    ny, nx, nz, nc = torus(groups, members)
    return pl.pallas_call(
        functools.partial(cross_kernel, groups, members),
        out_shape=jax.ShapeDtypeStruct((rows, units), BF16),
        in_specs=[WHOLE, ANY, ANY, ANY, WHOLE, WHOLE],
        out_specs=WHOLE,
        scratch_shapes=[
            VMEM(down.shape, BF16),
            VMEM(up.shape, BF16),
            VMEM((ny, nx, nz, nc, 2, depth, units), BF16),
            VMEM((steps, members, share, rank), BF16),
            VMEM((steps, members - 1, share, rank), BF16),
            VMEM((steps, members, share, rank), BF16),
            VMEM((rows, cols), BF16),
            VMEM((rows, units), F32),
            VMEM((GROUPS, members - 1, height, units), BF16),
            VMEM((GROUPS, members - 1, height, units), BF16),
            DMA((2 * layers + 2,)),
            DMA((phases, members - 1)),
            DMA((phases, members - 1)),
            DMA((9,)),
            DMA((9,)),
        ],
        compiler_params=pltpu.CompilerParams(
            collective_id=1, has_side_effects=True, vmem_limit_bytes=48 * 1024 * 1024
        ),
        name="cross",
    )(emb, quarter, down, up, bias, tower_bias)


def body(groups, members, feature_ids, tables, table_of_feature, cross_down, cross_up, cross_bias, tower_weight, tower_bias):
    m = lax.axis_index("mp")
    _, batch, hots = feature_ids.shape
    rows = batch // (groups * members)
    parts = max(1, LANES // rows)
    tiles = jnp.transpose(jnp.transpose(feature_ids[0]).reshape(hots, batch // LANES, LANES), (1, 0, 2))
    tiles = tiles.reshape(groups, members // parts, hots, LANES)
    own_ids = lax.dynamic_index_in_dim(tiles, m // parts, 1, keepdims=False).reshape(-1)
    depth, units = tower_weight.shape
    weight = tower_weight.reshape(2, depth // 2, units)
    emb, quarter = regrouped(own_ids, table_of_feature, tables[0], weight, groups, members, hots, rows)
    emb = emb.reshape(members * rows, -1)
    return crossed_and_towered(
        emb, quarter, cross_down, cross_up, cross_bias, tower_bias.reshape(1, -1), groups, members
    )


def solution(mesh):
    groups, members = mesh.shape["dp"], mesh.shape["mp"]
    return jax.shard_map(
        functools.partial(body, groups, members),
        mesh=mesh,
        in_specs=(
            P("dp", None, None),
            P("dp", None, None),
            P(),
            P(None, "mp", None),
            P(None, "mp", None),
            P(None, "mp"),
            P("dp", "mp"),
            P("mp"),
        ),
        out_specs=P("dp", "mp"),
        check_vma=False,
    )
```

time: 488 us -> 128 us (0.26)
  waiting for transfers between devices: 237 us -> 0 us
  local copies, waits for them, and re-layouts: 130 us -> 6.31 us
  Pallas kernels: 0 us -> 121 us
  blocking collectives: 62.9 us -> 0 us
  matrix products: 15.5 us -> 0 us
  between operations: 13.7 us -> 0.03 us
  other arithmetic: 13.3 us -> 0 us
  starting transfers between devices: 13.2 us -> 0 us
    all_gather x2 -> x0, waiting for transfers between devices: 195 us -> none  [the longest x1 126 us: body(): lax.all_gather(tower_weight, 'dp', axis=0, tiled=True)]
    pallas_call x0 -> x2, Pallas kernels: none -> 121 us  [the longest x1 60.8 us: regrouped(): pl.pallas_call(functools.partial(regroup_kernel, groups, members, hots),...]
    gather x9 -> x0, local copies, waits for them, and re-layouts: 116 us -> none  [the longest x8 114 us: body(): jnp.take(tables[0], own_ids[:, hot_index], axis=0).astype(jnp.float32)]
    all_to_all x2 -> x0, blocking collectives: 62.9 us -> none  [the longest x1 34.6 us: body(): lax.all_to_all(ordered, 'mp', split_axis=1, concat_axis=0, tiled=True)]
    all_to_all x2 -> x0, waiting for transfers between devices: 41.9 us -> none  [the longest x1 24.8 us: from_everyone(): lax.all_to_all(jnp.broadcast_to(x[None], (length, *x.shape)), axis, 0, 0,...]
    dot_general x5 -> x0, matrix products: 15.5 us -> none  [the longest x1 7.69 us: body(): jnp.dot(full_rows, lax.all_gather(tower_weight, 'dp', axis=0, tiled=True)...]
    all_to_all x2 -> x0, starting transfers between devices: 13.1 us -> none  [the longest x1 9.56 us: body(): lax.all_to_all(pooled, 'dp', split_axis=0, concat_axis=1, tiled=True)]
    another operation x2 -> x0, other arithmetic: 12.5 us -> none  [body(): pooled = jnp.stack(columns, axis=1)]
  transfers between devices with their start and end apart: 4 -> 0, of which waited for: 4 -> 0; matrix products, arithmetic and copies ran while one was open for 0% -> 0% of each run, Pallas kernels for 0% -> 0%
where the time goes in v2:
time: 128 us; the launch traced here: 127 us
  Pallas kernels  121 us (95%)
  local copies, waits for them, and re-layouts  6.31 us (5%)
    pallas_call x1, Pallas kernels, regrouped(): pl.pallas_call(functools.partial(regroup_kernel, groups, members, hots),...  60.8 us
    pallas_call x1, Pallas kernels, crossed_and_towered(): pl.pallas_call(functools.partial(cross_kernel, groups, members), out_shap...  59.8 us
    unnamed x11, local copies, waits for them, and re-layouts  5.59 us

profile of v2, /device:TPU:2, one launch (start us, length us, event | category | flops | bytes accessed | tf_op | source)
XLA Modules:
  0.0 126.9 jit_solution(5545377826176061701)
XLA Ops:
  0.0 0.0 copy-start
  0.0 1.0 copy-done
  1.0 0.7 dynamic-slice_bitcast_fusion.ids_hbm
  1.8 60.8 %regroup.1 = (bf16[4,64,2048]{2,1,0:T(8,128)(2,1)}, bf16[2,4,2,64,512]{4,3,2,1,0:T(8,128)(2,1)}) custom-call(s32[65536]{0:T(1024)} %dynamic-slice_bitcast_fusion.ids_hbm, s32[64]{0:T(128)} %order_ref.1, bf16[4096,128]{1,0:T(8,128)(2,1)} %bitcast.18, bf16[2,64,512]{2,1,0:T(8,128)(2,1)} %bitcast.19), custom_call_target="tpu_custom_call" | custom-call | tf_op jit(solution)/shard_map/regroup/pallas_call | solution.py:244
  62.6 0.0 copy-start.1
  62.6 1.2 copy-done.1
  63.8 0.0 copy-start.2
  63.8 1.2 copy-done.2
  65.1 0.0 copy-start.3
  65.1 0.7 copy-done.3
  65.8 0.0 copy-start.4
  65.8 0.7 copy-done.4
  66.5 59.8 %cross.1 = bf16[256,512]{1,0:T(8,128)(2,1)S(1)} custom-call(bf16[256,2048]{1,0:T(8,128)(2,1)S(1)} %bitcast.16, bf16[2,4,2,64,512]{4,3,2,1,0:T(8,128)(2,1)S(1)} %copy-done.2, bf16[2,2048,512]{2,1,0:T(8,128)(2,1)} %down_hbm.1, bf16[2,2048,512]{2,1,0:T(8,128)(2,1)} %up_hbm.1, f32[2,2048]{1,0:T(2,128)S(1)} %copy-done.3, f32[1,512]{1,0:T(1,128)S(1)} %bitcast.17), custom_call_target="tpu_custom_call" | custom-call | tf_op jit(solution)/shard_map/cross/pallas_call | solution.py:486
  126.2 0.7 copy.10
Async XLA Ops:
  0.0 1.0 copy-start
  62.6 1.2 copy-start.1
  63.8 1.2 copy-start.2
  65.1 0.7 copy-start.3
  65.8 0.7 copy-start.4

commit v3 on v2

v3 whole, which is shorter than its diff:
```python
import functools

import jax
import jax.numpy as jnp
from jax import lax
from jax.experimental import pallas as pl
from jax.experimental.pallas import tpu as pltpu
from jax.sharding import PartitionSpec as P

MESH = pl.DeviceIdType.MESH
VMEM = pltpu.VMEM
DMA = pltpu.SemaphoreType.DMA
F32 = jnp.float32
BF16 = jnp.bfloat16
WHOLE = pl.BlockSpec(memory_space=pltpu.VMEM)
SCALARS = pl.BlockSpec(memory_space=pltpu.SMEM)
ANY = pl.BlockSpec(memory_space=pl.ANY)
LANES = 128
CHUNKS = 4
GROUPS = 2


def torus(groups, members):
    rest = groups // members
    across = min(4, rest)
    rest //= across
    below = min(2, rest)
    return members, across, below, rest // below


def place(sizes, d):
    _, nx, nz, nc = sizes
    return d // (nx * nz * nc), lax.rem(d // (nz * nc), nx), lax.rem(d // nc, nz), lax.rem(d, nc)


def index_of(sizes, y, x, z, c):
    _, nx, nz, nc = sizes
    return ((y * nx + x) * nz + z) * nc + c


def signal(device):
    pl.semaphore_signal(pltpu.get_barrier_semaphore(), inc=1, device_id=device, device_id_type=MESH)


def remote(src, dst, send, recv, device):
    return pltpu.make_async_remote_copy(
        src_ref=src, dst_ref=dst, send_sem=send, recv_sem=recv, device_id=device, device_id_type=MESH
    )


def kernel(
    groups, members, hots, ids_hbm, order_ref, table_hbm, weight_hbm, down_hbm, up_hbm, bias_hbm, tower_bias_hbm,
    out_ref, ids_ref, table_ref, wide, acc, pooled, recv, packed, emb_ref, mine, quarter_ref, tower_ref,
    down_ref, up_ref, bias_ref, tower_bias_ref, part, arrived, proj, crossed, sums, partial_units, units_in,
    load_sem, dp_send, dp_recv, mp_send, mp_recv, send_sem, recv_sem, w_send, w_recv,
):
    d = lax.axis_index("dp")
    m = lax.axis_index("mp")
    vocab, width = table_ref.shape
    chunk = pooled.shape[2]
    per = groups // members
    rows, cols = emb_ref.shape
    layers, _, rank = down_ref.shape
    height = rows // GROUPS
    share = height // members
    units = out_ref.shape[1]
    sizes = torus(groups, members)
    ny, nx, nz, nc = sizes
    y, x, z, c = place(sizes, d)

    def start(copies):
        for copy in copies:
            copy.start()

    def wait(copies):
        for copy in copies:
            copy.wait()

    pairs = [(ids_hbm, ids_ref), (table_hbm, table_ref), (bias_hbm, bias_ref), (tower_bias_hbm, tower_bias_ref)]
    for layer in range(layers):
        pairs.append((down_hbm.at[layer], down_ref.at[layer]))
        pairs.append((up_hbm.at[layer], up_ref.at[layer]))
    loads = [pltpu.make_async_copy(a, b, load_sem.at[i]) for i, (a, b) in enumerate(pairs)]
    own_weight = pltpu.make_async_copy(weight_hbm, mine, load_sem.at[len(pairs)])
    start(loads[:2])

    def dp_at(k):
        return (lax.rem(d + k, groups), m)

    def mp_at(k):
        return (d, lax.rem(m + k, members))

    turned = (m * per + lax.rem(d, per), d // per)
    moved = d // per != m
    for count, device in ((groups, dp_at), (members, mp_at)):

        def greet(k, carry, device=device):
            signal(device(k))
            return carry

        lax.fori_loop(1, count, greet, 0)

    @pl.when(moved)
    def _():
        signal(turned)

    loads[1].wait()
    step = 256

    def widen(i, carry):
        at = pl.ds(pl.multiple_of(i * step, step), step)
        wide[at, :] = table_ref[at, :].astype(F32)
        return carry

    lax.fori_loop(0, vocab // step, widen, 0)
    loads[0].wait()

    local = CHUNKS * chunk
    parts_in_tile = LANES // local if local < LANES else 1
    lane0 = lax.rem(m, parts_in_tile) * local
    span = hots * LANES

    def lookups(ch, g):
        base = g * span + lane0

        def row(h, j):
            skipped = h * LANES + ch * chunk + j
            return wide[pl.ds(ids_ref.at[pl.ds(skipped, ids_ref.shape[0] - skipped)][base], 1), :]

        for j in range(chunk):
            total = row(0, j)
            for h in range(1, hots):
                total = total + row(h, j)
            acc[j : j + 1, :] = total

    def dp_copy(ch, k):
        return remote(
            pooled.at[ch, lax.rem(d + k, groups)], recv[ch].at[d], dp_send.at[ch], dp_recv.at[ch], dp_at(k)
        )

    def every(ch):
        some = pl.ds(0, groups - 1)
        return remote(pooled.at[ch, some], recv[ch].at[some], dp_send.at[ch], dp_recv.at[ch], dp_at(1))

    def blocks(ch, low, high, send=True):
        def block(k, carry):
            pooled[ch, lax.rem(d + k - 1, groups)] = acc[...].astype(BF16)
            lookups(ch, lax.rem(d + k, groups))
            if send:
                dp_copy(ch, k - 1).start()
            return carry

        lax.fori_loop(low, high, block, 0)

    def last_block(ch):
        pooled[ch, lax.rem(d + groups - 1, groups)] = acc[...].astype(BF16)
        lookups(ch, d)
        dp_copy(ch, groups - 1).start()
        recv[ch][d] = acc[...].astype(BF16)

    def emb_rows(ch, member):
        return pl.ds(pl.multiple_of((ch * members + member) * chunk, chunk), chunk)

    def mp_copy(ch, k):
        to = lax.rem(m + k, members)
        return remote(
            packed.at[ch, to], emb_ref.at[emb_rows(ch, m)], mp_send.at[ch, k - 1], mp_recv.at[ch, k - 1], mp_at(k)
        )

    def spread(ch):
        every(ch).wait_recv()
        for p in range(groups):
            packed[ch, p // per, :, (p % per) * width : (p % per + 1) * width] = recv[ch][order_ref[p]]
        for k in range(1, members):
            mp_copy(ch, k).start()
        emb_ref[emb_rows(ch, m), :] = packed[ch, m]

    swap = remote(weight_hbm, mine, w_send.at[0], w_recv.at[0], turned)
    right, left = lax.rem(x + 1, nx), lax.rem(x + nx - 1, nx)
    upper, lower = lax.rem(y + 1, ny), lax.rem(y + ny - 1, ny)
    depth = mine.shape[1]
    first, second = pl.ds(0, depth // 2), pl.ds(depth // 2, depth // 2)

    def at(y, x, z, c):
        return (index_of(sizes, y, x, z, c), m)

    to_right, to_left = at(y, right, z, c), at(y, left, z, c)
    to_upper, to_lower = at(upper, x, z, c), at(lower, x, z, c)

    def send_all(number, moves):
        return [
            remote(src, dst, w_send.at[number + i], w_recv.at[number + i], device)
            for i, (src, dst, device) in enumerate(moves)
        ]

    def below():
        if nz == 1:
            return []
        to = at(y, x, 1 - z, c)
        return send_all(1, [(mine.at[0], quarter_ref.at[0, x, z], to), (mine.at[1], quarter_ref.at[1, y, z], to)])

    def beside():
        own = quarter_ref.at[1, y]
        moves = [(own, own, to_upper), (own, own, to_lower)]
        if nx > 1:
            own = quarter_ref.at[0, x]
            moves += [(own, own, to_right), (own, own, to_left)]
        return send_all(3, moves)

    def relayed():
        a, b = quarter_ref.at[1, lower, :, first], quarter_ref.at[1, upper, :, second]
        moves = [(a, a, to_upper), (b, b, to_lower)]
        if nx > 1:
            a, b = quarter_ref.at[0, left, :, first], quarter_ref.at[0, right, :, second]
            moves += [(a, a, to_right), (b, b, to_left)]
        return send_all(7, moves)

    def first_way():
        src, to = quarter_ref.at[0, pl.ds(0, nx)], tower_ref.at[y, :, :, c, 0]
        moves = [(src, to, to_upper), (src, to, to_lower)]
        if nx > 1:
            src, to = quarter_ref.at[1, pl.ds(0, ny)], tower_ref.at[:, x, :, c, 1]
            moves += [(src, to, to_right), (src, to, to_left)]
        return send_all(11, moves)

    def second_way():
        a, b = tower_ref.at[lower, :, :, c, 0, first], tower_ref.at[upper, :, :, c, 0, second]
        moves = [(a, a, to_upper), (b, b, to_lower)]
        if nx > 1:
            a, b = tower_ref.at[:, left, :, c, 1, first], tower_ref.at[:, right, :, c, 1, second]
            moves += [(a, a, to_right), (b, b, to_left)]
        return send_all(15, moves)

    def pair():
        if nc == 1:
            return []
        both = tower_ref.at[:, :, :, c]
        return send_all(19, [(both, both, at(y, x, z, 1 - c))])

    def rows_of(g):
        return pl.ds(g * height, height)

    def scatter(layer, g):
        i = layer * GROUPS + g
        return [
            remote(
                part.at[i, lax.rem(m + k, members)],
                arrived.at[i, k - 1],
                send_sem.at[2 * i, k - 1],
                recv_sem.at[2 * i, k - 1],
                mp_at(k),
            )
            for k in range(1, members)
        ]

    def gather(layer, g):
        i = layer * GROUPS + g
        return [
            remote(
                proj.at[i, m], proj.at[i, m], send_sem.at[2 * i + 1, k - 1], recv_sem.at[2 * i + 1, k - 1], mp_at(k)
            )
            for k in range(1, members)
        ]

    def project(layer, g):
        source = emb_ref if layer == 0 else crossed
        product = jnp.dot(source[rows_of(g), :], down_ref[layer], preferred_element_type=F32)
        i = layer * GROUPS + g
        part[i] = product.astype(BF16).reshape(members, share, rank)
        start(scatter(layer, g))

    def add_up(layer, g):
        i = layer * GROUPS + g
        wait(scatter(layer, g))
        total = part[i, m].astype(F32)
        for k in range(1, members):
            total = total + arrived[i, k - 1].astype(F32)
        proj[i, m] = total.astype(BF16)
        start(gather(layer, g))

    tile = min(512, cols)

    def lift(layer, g):
        i = layer * GROUPS + g
        wait(gather(layer, g))
        source = emb_ref if layer == 0 else crossed
        projected = proj[i].reshape(height, rank)
        here = rows_of(g)

        def columns(j, carry):
            at = pl.ds(pl.multiple_of(j * tile, tile), tile)
            lifted = lax.dot_general(
                projected, up_ref[layer, at, :], (((1,), (1,)), ((), ())), preferred_element_type=F32
            )
            value = emb_ref[here, at].astype(F32) * (lifted + bias_ref[layer : layer + 1, at])
            crossed[here, at] = (value + source[here, at].astype(F32)).astype(BF16)
            return carry

        lax.fori_loop(0, cols // tile, columns, 0)

    def tower(g, block):
        weights = tower_ref[block].reshape(cols, units)
        return jnp.dot(crossed[rows_of(g), :], weights, preferred_element_type=F32)

    def exchange(g, k):
        i = 2 * layers * GROUPS + g
        return remote(
            partial_units.at[g, k - 1], units_in.at[g, k - 1], send_sem.at[i, k - 1], recv_sem.at[i, k - 1], mp_at(k)
        )

    in_group = CHUNKS // GROUPS

    def project_first(g):
        for ch in range(g * in_group, (g + 1) * in_group):
            for k in range(1, members):
                mp_copy(ch, k).wait_recv()
        project(0, g)

    cuts = [2, 2 + groups // 4, 1 + groups // 2, 1 + 3 * groups // 4, groups]

    lookups(0, lax.rem(d + 1, groups))
    blocks(0, cuts[0], cuts[2], send=False)
    pl.semaphore_wait(
        pltpu.get_barrier_semaphore(), groups + members - 2 + jnp.where(moved, 1, 0).astype(jnp.int32)
    )

    def send_first(k, carry):
        dp_copy(0, k).start()
        return carry

    lax.fori_loop(1, cuts[2] - 1, send_first, 0)

    @pl.when(moved)
    def _():
        swap.start()

    @pl.when(jnp.logical_not(moved))
    def _():
        own_weight.start()

    blocks(0, cuts[2], cuts[4])
    last_block(0)
    start(loads[2:])

    @pl.when(moved)
    def _():
        swap.wait()

    @pl.when(jnp.logical_not(moved))
    def _():
        own_weight.wait()

    start(below())
    quarter_ref[0, x, z] = mine[0]
    quarter_ref[1, y, z] = mine[1]
    for ch in range(1, CHUNKS):
        lookups(ch, lax.rem(d + 1, groups))
        blocks(ch, cuts[0], cuts[3])
        spread(ch - 1)
        if ch == 1:
            wait(below())
            start(beside())
        if ch == 2:
            wait(beside())
            start(relayed())
        if ch == 3:
            wait(relayed())
            start(first_way())
        blocks(ch, cuts[3], cuts[4])
        last_block(ch)
    for load in loads[2:]:
        load.wait()
    project_first(0)
    spread(CHUNKS - 1)
    tower_ref[y, :, :, c, 0] = quarter_ref[0, :nx]
    tower_ref[:, x, :, c, 1] = quarter_ref[1, :ny]
    add_up(0, 0)
    for g in range(1, GROUPS):
        project_first(g)
        add_up(0, g)
    wait(first_way())
    start(second_way())
    for layer in range(1, layers):
        for g in range(GROUPS):
            lift(layer - 1, g)
            project(layer, g)
        if layer == 1:
            wait(second_way())
            start(pair())
        for g in range(GROUPS):
            add_up(layer, g)
    for g in range(GROUPS):
        lift(layers - 1, g)
        if g == 0:
            wait(pair())

        def send_units(k, carry, g=g):
            partial_units[g, k - 1] = tower(g, lax.rem(m + k, members)).astype(BF16)
            exchange(g, k).start()
            return carry

        lax.fori_loop(1, members, send_units, 0)
        sums[rows_of(g), :] = tower(g, m) + tower_bias_ref[...]
    for g in range(GROUPS):
        total = sums[rows_of(g), :]
        for k in range(1, members):
            exchange(g, k).wait()
            total = total + units_in[g, k - 1].astype(F32)
        total = jnp.maximum(total, 0.0).astype(BF16)
        for ch in range(in_group):
            for member in range(members):
                to = (member * CHUNKS + g * in_group + ch) * chunk
                at0 = (ch * members + member) * chunk
                out_ref[to : to + chunk, :] = total[at0 : at0 + chunk, :]
    for ch in range(CHUNKS):
        every(ch).wait_send()
        for k in range(1, members):
            mp_copy(ch, k).wait_send()


def whole(ids, order, table, weight, down, up, bias, tower_bias, groups, members, hots, local):
    vocab, width = table.shape
    per = groups // members
    chunk = local // CHUNKS
    rows, cols = members * local, per * width
    layers, _, rank = down.shape
    depth, units = weight.shape[1:]
    height = rows // GROUPS
    share = height // members
    steps = layers * GROUPS
    phases = 2 * steps + GROUPS
    ny, nx, nz, nc = torus(groups, members)
    return pl.pallas_call(
        functools.partial(kernel, groups, members, hots),
        out_shape=jax.ShapeDtypeStruct((rows, units), BF16),
        in_specs=[ANY, SCALARS] + [ANY] * 6,
        out_specs=WHOLE,
        scratch_shapes=[
            pltpu.SMEM(ids.shape, jnp.int32),
            VMEM((vocab, width), BF16),
            VMEM((vocab, width), F32),
            VMEM((chunk, width), F32),
            VMEM((CHUNKS, groups, chunk, width), BF16),
            [VMEM((groups, chunk, width), BF16) for _ in range(CHUNKS)],
            VMEM((CHUNKS, members, chunk, cols), BF16),
            VMEM((rows, cols), BF16),
            VMEM((2, depth, units), BF16),
            VMEM((2, max(ny, nx), nz, depth, units), BF16),
            VMEM((ny, nx, nz, nc, 2, depth, units), BF16),
            VMEM(down.shape, BF16),
            VMEM(up.shape, BF16),
            VMEM(bias.shape, F32),
            VMEM(tower_bias.shape, F32),
            VMEM((steps, members, share, rank), BF16),
            VMEM((steps, members - 1, share, rank), BF16),
            VMEM((steps, members, share, rank), BF16),
            VMEM((rows, cols), BF16),
            VMEM((rows, units), F32),
            VMEM((GROUPS, members - 1, height, units), BF16),
            VMEM((GROUPS, members - 1, height, units), BF16),
            DMA((2 * layers + 5,)),
            DMA((CHUNKS,)),
            DMA((CHUNKS,)),
            DMA((CHUNKS, members - 1)),
            DMA((CHUNKS, members - 1)),
            DMA((phases, members - 1)),
            DMA((phases, members - 1)),
            DMA((20,)),
            DMA((20,)),
        ],
        compiler_params=pltpu.CompilerParams(
            collective_id=0, has_side_effects=True, vmem_limit_bytes=56 * 1024 * 1024
        ),
        name="whole",
    )(ids, order, table, weight, down, up, bias, tower_bias)


def body(groups, members, feature_ids, tables, table_of_feature, cross_down, cross_up, cross_bias, tower_weight, tower_bias):
    m = lax.axis_index("mp")
    _, batch, hots = feature_ids.shape
    rows = batch // (groups * members)
    parts = max(1, LANES // rows)
    tiles = jnp.transpose(jnp.transpose(feature_ids[0]).reshape(hots, batch // LANES, LANES), (1, 0, 2))
    tiles = tiles.reshape(groups, members // parts, hots, LANES)
    own_ids = lax.dynamic_index_in_dim(tiles, m // parts, 1, keepdims=False).reshape(-1)
    depth, units = tower_weight.shape
    weight = tower_weight.reshape(2, depth // 2, units)
    return whole(
        own_ids, table_of_feature, tables[0], weight, cross_down, cross_up, cross_bias,
        tower_bias.reshape(1, -1), groups, members, hots, rows,
    )


def solution(mesh):
    groups, members = mesh.shape["dp"], mesh.shape["mp"]
    return jax.shard_map(
        functools.partial(body, groups, members),
        mesh=mesh,
        in_specs=(
            P("dp", None, None),
            P("dp", None, None),
            P(),
            P(None, "mp", None),
            P(None, "mp", None),
            P(None, "mp"),
            P("dp", "mp"),
            P("mp"),
        ),
        out_specs=P("dp", "mp"),
        check_vma=False,
    )
```

time: 128 us -> 129 us (level)
  Pallas kernels: 121 us -> 124 us
  local copies, waits for them, and re-layouts: 6.31 us -> 3.43 us
    pallas_call x2 -> x1, Pallas kernels: 121 us -> 124 us  [whole(): pl.pallas_call(functools.partial(kernel, groups, members, hots), out_shap...]
    unnamed x11 -> x3, local copies, waits for them, and re-layouts: 5.59 us -> 2.71 us
where the time goes in v3:
time: 129 us; the launch traced here: 127 us
  Pallas kernels  124 us (96%)
  local copies, waits for them, and re-layouts  3.43 us (3%)
    pallas_call x1, Pallas kernels, whole(): pl.pallas_call(functools.partial(kernel, groups, members, hots), out_shap...  124 us
    unnamed x3, local copies, waits for them, and re-layouts  2.71 us

profile of v3, /device:TPU:2, one launch (start us, length us, event | category | flops | bytes accessed | tf_op | source)
XLA Modules:
  0.0 127.3 jit_solution(1598670275216222146)
XLA Ops:
  0.0 0.0 copy-start
  0.0 1.0 copy-done
  1.0 0.7 dynamic-slice_bitcast_fusion.ids_hbm
  1.8 123.9 %whole.1 = bf16[256,512]{1,0:T(8,128)(2,1)} custom-call(s32[65536]{0:T(1024)} %dynamic-slice_bitcast_fusion.ids_hbm, s32[64]{0:T(128)} %order_ref.1, bf16[4096,128]{1,0:T(8,128)(2,1)} %bitcast.15, bf16[2,64,512]{2,1,0:T(8,128)(2,1)} %bitcast.16, bf16[2,2048,512]{2,1,0:T(8,128)(2,1)} %down_hbm.1, bf16[2,2048,512]{2,1,0:T(8,128)(2,1)} %up_hbm.1, ...), custom_call_target="tpu_custom_call" | custom-call | tf_op jit(solution)/shard_map/whole/pallas_call | solution.py:433
  125.6 1.7 %copy.10 = bf16[256,512]{1,0:T(8,128)(2,1)} copy(bf16[256,512]{1,0:T(8,128)(2,1)} %whole.1) | data formatting | bytes 524288
Async XLA Ops:
  0.0 1.0 copy-start

commit v4 on v3

--- a/solution.py
+++ b/solution.py
@@ -51,7 +51,7 @@
 def kernel(
     groups, members, hots, ids_hbm, order_ref, table_hbm, weight_hbm, down_hbm, up_hbm, bias_hbm, tower_bias_hbm,
     out_ref, ids_ref, table_ref, wide, acc, pooled, recv, packed, emb_ref, mine, quarter_ref, tower_ref,
-    down_ref, up_ref, bias_ref, tower_bias_ref, part, arrived, proj, crossed, sums, partial_units, units_in,
+    down_ref, up_ref, bias_ref, tower_bias_ref, part, arrived, proj, crossed, sums, near_units, far_units, far_in, partial_units, units_in,
     load_sem, dp_send, dp_recv, mp_send, mp_recv, send_sem, recv_sem, w_send, w_recv,
 ):
     d = lax.axis_index("dp")
@@ -302,11 +302,36 @@
         weights = tower_ref[block].reshape(cols, units)
         return jnp.dot(crossed[rows_of(g), :], weights, preferred_element_type=F32)
 
-    def exchange(g, k):
-        i = 2 * layers * GROUPS + g
-        return remote(
-            partial_units.at[g, k - 1], units_in.at[g, k - 1], send_sem.at[i, k - 1], recv_sem.at[i, k - 1], mp_at(k)
-        )
+    tower_phase = 2 * layers * GROUPS
+    top, low = pl.ds(0, height // 2), pl.ds(height // 2, height // 2)
+
+    def opposite(g):
+        i = tower_phase + 2 * g
+        return [
+            remote(far_units.at[g, top], far_in.at[g, 0], send_sem.at[i, 0], recv_sem.at[i, 0], mp_at(1)),
+            remote(far_units.at[g, low], far_in.at[g, 1], send_sem.at[i, 1], recv_sem.at[i, 1], mp_at(members - 1)),
+        ]
+
+    def neighbours(g):
+        i = tower_phase + 2 * g + 1
+        return [
+            remote(partial_units.at[g, 0], units_in.at[g, 0], send_sem.at[i, 0], recv_sem.at[i, 0], mp_at(1)),
+            remote(partial_units.at[g, 1], units_in.at[g, 1], send_sem.at[i, 1], recv_sem.at[i, 1], mp_at(members - 1)),
+        ]
+
+    def send_far(g):
+        far_units[g] = tower(g, lax.rem(m + 2, members)).astype(BF16)
+        start(opposite(g))
+
+    def send_near(g):
+        for side, k in enumerate((1, members - 1)):
+            near_units[side] = tower(g, lax.rem(m + k, members))
+        wait(opposite(g))
+        partial_units[g, 0, top, :] = (near_units[0, top, :] + far_in[g, 0].astype(F32)).astype(BF16)
+        partial_units[g, 0, low, :] = near_units[0, low, :].astype(BF16)
+        partial_units[g, 1, top, :] = near_units[1, top, :].astype(BF16)
+        partial_units[g, 1, low, :] = (near_units[1, low, :] + far_in[g, 1].astype(F32)).astype(BF16)
+        start(neighbours(g))
 
     in_group = CHUNKS // GROUPS
 
@@ -357,21 +382,20 @@
         lookups(ch, lax.rem(d + 1, groups))
         blocks(ch, cuts[0], cuts[3])
         spread(ch - 1)
+        blocks(ch, cuts[3], cuts[4])
+        last_block(ch)
         if ch == 1:
             wait(below())
             start(beside())
         if ch == 2:
             wait(beside())
             start(relayed())
-        if ch == 3:
-            wait(relayed())
-            start(first_way())
-        blocks(ch, cuts[3], cuts[4])
-        last_block(ch)
     for load in loads[2:]:
         load.wait()
     project_first(0)
     spread(CHUNKS - 1)
+    wait(relayed())
+    start(first_way())
     tower_ref[y, :, :, c, 0] = quarter_ref[0, :nx]
     tower_ref[:, x, :, c, 1] = quarter_ref[1, :ny]
     add_up(0, 0)
@@ -393,19 +417,14 @@
         lift(layers - 1, g)
         if g == 0:
             wait(pair())
-
-        def send_units(k, carry, g=g):
-            partial_units[g, k - 1] = tower(g, lax.rem(m + k, members)).astype(BF16)
-            exchange(g, k).start()
-            return carry
-
-        lax.fori_loop(1, members, send_units, 0)
+        send_far(g)
+    for g in range(GROUPS):
+        send_near(g)
+    for g in range(GROUPS):
         sums[rows_of(g), :] = tower(g, m) + tower_bias_ref[...]
     for g in range(GROUPS):
-        total = sums[rows_of(g), :]
-        for k in range(1, members):
-            exchange(g, k).wait()
-            total = total + units_in[g, k - 1].astype(F32)
+        wait(neighbours(g))
+        total = sums[rows_of(g), :] + units_in[g, 0].astype(F32) + units_in[g, 1].astype(F32)
         total = jnp.maximum(total, 0.0).astype(BF16)
         for ch in range(in_group):
             for member in range(members):
@@ -428,7 +447,7 @@
     height = rows // GROUPS
     share = height // members
     steps = layers * GROUPS
-    phases = 2 * steps + GROUPS
+    phases = 2 * steps + 2 * GROUPS
     ny, nx, nz, nc = torus(groups, members)
     return pl.pallas_call(
         functools.partial(kernel, groups, members, hots),
@@ -456,8 +475,11 @@
             VMEM((steps, members, share, rank), BF16),
             VMEM((rows, cols), BF16),
             VMEM((rows, units), F32),
-            VMEM((GROUPS, members - 1, height, units), BF16),
-            VMEM((GROUPS, members - 1, height, units), BF16),
+            VMEM((2, height, units), F32),
+            VMEM((GROUPS, height, units), BF16),
+            VMEM((GROUPS, 2, height // 2, units), BF16),
+            VMEM((GROUPS, 2, height, units), BF16),
+            VMEM((GROUPS, 2, height, units), BF16),
             DMA((2 * layers + 5,)),
             DMA((CHUNKS,)),
             DMA((CHUNKS,)),

time: 129 us -> 119 us (0.922)
  Pallas kernels: 124 us -> 114 us
    pallas_call x1, Pallas kernels: 124 us -> 114 us  [whole(): pl.pallas_call(functools.partial(kernel, groups, members, hots), out_shap...]
where the time goes in v4:
time: 119 us; the launch traced here: 117 us
  Pallas kernels  114 us (96%)
  local copies, waits for them, and re-layouts  3.43 us (3%)
    pallas_call x1, Pallas kernels, whole(): pl.pallas_call(functools.partial(kernel, groups, members, hots), out_shap...  114 us
    unnamed x3, local copies, waits for them, and re-layouts  2.71 us

profile of v4, /device:TPU:2, one launch (start us, length us, event | category | flops | bytes accessed | tf_op | source)
XLA Modules:
  0.0 117.2 jit_solution(5883043192789697936)
XLA Ops:
  0.0 0.0 copy-start
  0.0 1.0 copy-done
  1.0 0.7 dynamic-slice_bitcast_fusion.ids_hbm
  1.8 113.8 %whole.1 = bf16[256,512]{1,0:T(8,128)(2,1)} custom-call(s32[65536]{0:T(1024)} %dynamic-slice_bitcast_fusion.ids_hbm, s32[64]{0:T(128)} %order_ref.1, bf16[4096,128]{1,0:T(8,128)(2,1)} %bitcast.15, bf16[2,64,512]{2,1,0:T(8,128)(2,1)} %bitcast.16, bf16[2,2048,512]{2,1,0:T(8,128)(2,1)} %down_hbm.1, bf16[2,2048,512]{2,1,0:T(8,128)(2,1)} %up_hbm.1, ...), custom_call_target="tpu_custom_call" | custom-call | tf_op jit(solution)/shard_map/whole/pallas_call | solution.py:452
  115.6 1.7 %copy.10 = bf16[256,512]{1,0:T(8,128)(2,1)} copy(bf16[256,512]{1,0:T(8,128)(2,1)} %whole.1) | data formatting | bytes 524288
Async XLA Ops:
  0.0 1.0 copy-start

commit v5 on v4

--- a/solution.py
+++ b/solution.py
@@ -133,29 +133,44 @@
                 total = total + row(h, j)
             acc[j : j + 1, :] = total
 
-    def dp_copy(ch, k):
-        return remote(
-            pooled.at[ch, lax.rem(d + k, groups)], recv[ch].at[d], dp_send.at[ch], dp_recv.at[ch], dp_at(k)
+    def target(k):
+        if nz == 1:
+            return lax.rem(d + k, groups)
+        flat = groups // nz
+        across = 1 - (k - 1) // flat
+        u = lax.rem(k - 1, flat) + 1 - across
+        return index_of(
+            sizes, lax.rem(y + u // (nx * nc), ny), lax.rem(x + lax.rem(u // nc, nx), nx),
+            lax.rem(z + across, nz), lax.rem(c + lax.rem(u, nc), nc),
         )
+
+    def dp_copy(ch, g):
+        return remote(pooled.at[ch, g], recv[ch].at[d], dp_send.at[ch], dp_recv.at[ch], (g, m))
 
     def every(ch):
         some = pl.ds(0, groups - 1)
         return remote(pooled.at[ch, some], recv[ch].at[some], dp_send.at[ch], dp_recv.at[ch], dp_at(1))
 
-    def blocks(ch, low, high, send=True):
-        def block(k, carry):
-            pooled[ch, lax.rem(d + k - 1, groups)] = acc[...].astype(BF16)
-            lookups(ch, lax.rem(d + k, groups))
+    def first_block(ch):
+        g = target(jnp.int32(1))
+        lookups(ch, g)
+        return g
+
+    def blocks(ch, low, high, before, send=True):
+        def block(k, before):
+            pooled[ch, before] = acc[...].astype(BF16)
+            now = target(k)
+            lookups(ch, now)
             if send:
-                dp_copy(ch, k - 1).start()
-            return carry
-
-        lax.fori_loop(low, high, block, 0)
-
-    def last_block(ch):
-        pooled[ch, lax.rem(d + groups - 1, groups)] = acc[...].astype(BF16)
+                dp_copy(ch, before).start()
+            return now
+
+        return lax.fori_loop(low, high, block, before)
+
+    def last_block(ch, before):
+        pooled[ch, before] = acc[...].astype(BF16)
         lookups(ch, d)
-        dp_copy(ch, groups - 1).start()
+        dp_copy(ch, before).start()
         recv[ch][d] = acc[...].astype(BF16)
 
     def emb_rows(ch, member):
@@ -343,14 +358,13 @@
 
     cuts = [2, 2 + groups // 4, 1 + groups // 2, 1 + 3 * groups // 4, groups]
 
-    lookups(0, lax.rem(d + 1, groups))
-    blocks(0, cuts[0], cuts[2], send=False)
+    before = blocks(0, cuts[0], cuts[2], first_block(0), send=False)
     pl.semaphore_wait(
         pltpu.get_barrier_semaphore(), groups + members - 2 + jnp.where(moved, 1, 0).astype(jnp.int32)
     )
 
     def send_first(k, carry):
-        dp_copy(0, k).start()
+        dp_copy(0, target(k)).start()
         return carry
 
     lax.fori_loop(1, cuts[2] - 1, send_first, 0)
@@ -363,8 +377,7 @@
     def _():
         own_weight.start()
 
-    blocks(0, cuts[2], cuts[4])
-    last_block(0)
+    last_block(0, blocks(0, cuts[2], cuts[4], before))
     start(loads[2:])
 
     @pl.when(moved)
@@ -379,11 +392,9 @@
     quarter_ref[0, x, z] = mine[0]
     quarter_ref[1, y, z] = mine[1]
     for ch in range(1, CHUNKS):
-        lookups(ch, lax.rem(d + 1, groups))
-        blocks(ch, cuts[0], cuts[3])
+        before = blocks(ch, cuts[0], cuts[3], first_block(ch))
         spread(ch - 1)
-        blocks(ch, cuts[3], cuts[4])
-        last_block(ch)
+        last_block(ch, blocks(ch, cuts[3], cuts[4], before))
         if ch == 1:
             wait(below())
             start(beside())

time: 119 us -> 117 us (0.983)
  no operation moved by 1% of the time
where the time goes in v5:
time: 117 us; the launch traced here: 116 us
  Pallas kernels  113 us (97%)
  local copies, waits for them, and re-layouts  3.43 us (3%)
    pallas_call x1, Pallas kernels, whole(): pl.pallas_call(functools.partial(kernel, groups, members, hots), out_shap...  113 us
    unnamed x3, local copies, waits for them, and re-layouts  2.71 us

profile of v5, /device:TPU:2, one launch (start us, length us, event | category | flops | bytes accessed | tf_op | source)
XLA Modules:
  0.0 116.3 jit_solution(3600590571017726586)
XLA Ops:
  0.0 0.0 copy-start
  0.0 1.0 copy-done
  1.0 0.7 dynamic-slice_bitcast_fusion.ids_hbm
  1.8 112.8 %whole.1 = bf16[256,512]{1,0:T(8,128)(2,1)} custom-call(s32[65536]{0:T(1024)} %dynamic-slice_bitcast_fusion.ids_hbm, s32[64]{0:T(128)} %order_ref.1, bf16[4096,128]{1,0:T(8,128)(2,1)} %bitcast.15, bf16[2,64,512]{2,1,0:T(8,128)(2,1)} %bitcast.16, bf16[2,2048,512]{2,1,0:T(8,128)(2,1)} %down_hbm.1, bf16[2,2048,512]{2,1,0:T(8,128)(2,1)} %up_hbm.1, ...), custom_call_target="tpu_custom_call" | custom-call | tf_op jit(solution)/shard_map/whole/pallas_call | solution.py:463
  114.6 1.7 %copy.10 = bf16[256,512]{1,0:T(8,128)(2,1)} copy(bf16[256,512]{1,0:T(8,128)(2,1)} %whole.1) | data formatting | bytes 524288
Async XLA Ops:
  0.0 1.0 copy-start

commit v6 on v5

--- a/solution.py
+++ b/solution.py
@@ -68,6 +68,8 @@
     ny, nx, nz, nc = sizes
     y, x, z, c = place(sizes, d)
 
+    far_first = sorted(range(1, members), key=lambda k: -min(k, members - k))
+
     def start(copies):
         for copy in copies:
             copy.start()
@@ -186,7 +188,7 @@
         every(ch).wait_recv()
         for p in range(groups):
             packed[ch, p // per, :, (p % per) * width : (p % per + 1) * width] = recv[ch][order_ref[p]]
-        for k in range(1, members):
+        for k in far_first:
             mp_copy(ch, k).start()
         emb_ref[emb_rows(ch, m), :] = packed[ch, m]
 
@@ -265,7 +267,7 @@
                 recv_sem.at[2 * i, k - 1],
                 mp_at(k),
             )
-            for k in range(1, members)
+            for k in far_first
         ]
 
     def gather(layer, g):
@@ -274,7 +276,7 @@
             remote(
                 proj.at[i, m], proj.at[i, m], send_sem.at[2 * i + 1, k - 1], recv_sem.at[2 * i + 1, k - 1], mp_at(k)
             )
-            for k in range(1, members)
+            for k in far_first
         ]
 
     def project(layer, g):
@@ -358,7 +360,7 @@
 
     cuts = [2, 2 + groups // 4, 1 + groups // 2, 1 + 3 * groups // 4, groups]
 
-    before = blocks(0, cuts[0], cuts[2], first_block(0), send=False)
+    before = blocks(0, cuts[0], cuts[1], first_block(0), send=False)
     pl.semaphore_wait(
         pltpu.get_barrier_semaphore(), groups + members - 2 + jnp.where(moved, 1, 0).astype(jnp.int32)
     )
@@ -367,7 +369,7 @@
         dp_copy(0, target(k)).start()
         return carry
 
-    lax.fori_loop(1, cuts[2] - 1, send_first, 0)
+    lax.fori_loop(1, cuts[1] - 1, send_first, 0)
 
     @pl.when(moved)
     def _():
@@ -377,7 +379,7 @@
     def _():
         own_weight.start()
 
-    last_block(0, blocks(0, cuts[2], cuts[4], before))
+    last_block(0, blocks(0, cuts[1], cuts[4], before))
     start(loads[2:])
 
     @pl.when(moved)

time: 117 us -> 113 us (0.966)
  Pallas kernels: 113 us -> 108 us
    pallas_call x1, Pallas kernels: 113 us -> 108 us  [whole(): pl.pallas_call(functools.partial(kernel, groups, members, hots), out_shap...]
where the time goes in v6:
time: 113 us; the launch traced here: 111 us
  Pallas kernels  108 us (96%)
  local copies, waits for them, and re-layouts  3.43 us (3%)
    pallas_call x1, Pallas kernels, whole(): pl.pallas_call(functools.partial(kernel, groups, members, hots), out_shap...  108 us
    unnamed x3, local copies, waits for them, and re-layouts  2.71 us

profile of v6, /device:TPU:2, one launch (start us, length us, event | category | flops | bytes accessed | tf_op | source)
XLA Modules:
  0.0 111.2 jit_solution(7194300938340220699)
XLA Ops:
  0.0 0.0 copy-start
  0.0 1.0 copy-done
  1.0 0.7 dynamic-slice_bitcast_fusion.ids_hbm
  1.8 107.8 %whole.1 = bf16[256,512]{1,0:T(8,128)(2,1)} custom-call(s32[65536]{0:T(1024)} %dynamic-slice_bitcast_fusion.ids_hbm, s32[64]{0:T(128)} %order_ref.1, bf16[4096,128]{1,0:T(8,128)(2,1)} %bitcast.15, bf16[2,64,512]{2,1,0:T(8,128)(2,1)} %bitcast.16, bf16[2,2048,512]{2,1,0:T(8,128)(2,1)} %down_hbm.1, bf16[2,2048,512]{2,1,0:T(8,128)(2,1)} %up_hbm.1, ...), custom_call_target="tpu_custom_call" | custom-call | tf_op jit(solution)/shard_map/whole/pallas_call | solution.py:465
  109.5 1.7 %copy.10 = bf16[256,512]{1,0:T(8,128)(2,1)} copy(bf16[256,512]{1,0:T(8,128)(2,1)} %whole.1) | data formatting | bytes 524288
Async XLA Ops:
  0.0 1.0 copy-start

commit v7 on v6

--- a/solution.py
+++ b/solution.py
@@ -358,9 +358,10 @@
                 mp_copy(ch, k).wait_recv()
         project(0, g)
 
+    early = 2 + groups // 16
     cuts = [2, 2 + groups // 4, 1 + groups // 2, 1 + 3 * groups // 4, groups]
 
-    before = blocks(0, cuts[0], cuts[1], first_block(0), send=False)
+    before = blocks(0, cuts[0], early, first_block(0), send=False)
     pl.semaphore_wait(
         pltpu.get_barrier_semaphore(), groups + members - 2 + jnp.where(moved, 1, 0).astype(jnp.int32)
     )
@@ -369,7 +370,7 @@
         dp_copy(0, target(k)).start()
         return carry
 
-    lax.fori_loop(1, cuts[1] - 1, send_first, 0)
+    lax.fori_loop(1, early - 1, send_first, 0)
 
     @pl.when(moved)
     def _():
@@ -379,7 +380,7 @@
     def _():
         own_weight.start()
 
-    last_block(0, blocks(0, cuts[1], cuts[4], before))
+    last_block(0, blocks(0, early, cuts[4], before))
     start(loads[2:])
 
     @pl.when(moved)

time: 113 us -> 111 us (0.982)
  the two profiles are of different devices: /device:TPU:2 before, /device:TPU:20 now
where the time goes in v7:
time: 111 us
  Pallas kernels  108 us (97%)
  local copies, waits for them, and re-layouts  3.43 us (3%)
    pallas_call x1, Pallas kernels, whole(): pl.pallas_call(functools.partial(kernel, groups, members, hots), out_shap...  108 us
    unnamed x3, local copies, waits for them, and re-layouts  2.71 us

profile of v7, /device:TPU:20, one launch (start us, length us, event | category | flops | bytes accessed | tf_op | source)
XLA Modules:
  0.0 111.0 jit_solution(5772953206140261738)
XLA Ops:
  0.0 0.0 copy-start
  0.0 1.0 copy-done
  1.0 0.7 dynamic-slice_bitcast_fusion.ids_hbm
  1.8 107.6 %whole.1 = bf16[256,512]{1,0:T(8,128)(2,1)} custom-call(s32[65536]{0:T(1024)} %dynamic-slice_bitcast_fusion.ids_hbm, s32[64]{0:T(128)} %order_ref.1, bf16[4096,128]{1,0:T(8,128)(2,1)} %bitcast.15, bf16[2,64,512]{2,1,0:T(8,128)(2,1)} %bitcast.16, bf16[2,2048,512]{2,1,0:T(8,128)(2,1)} %down_hbm.1, bf16[2,2048,512]{2,1,0:T(8,128)(2,1)} %up_hbm.1, ...), custom_call_target="tpu_custom_call" | custom-call | tf_op jit(solution)/shard_map/whole/pallas_call | solution.py:466
  109.3 1.7 %copy.10 = bf16[256,512]{1,0:T(8,128)(2,1)} copy(bf16[256,512]{1,0:T(8,128)(2,1)} %whole.1) | data formatting | bytes 524288
Async XLA Ops:
  0.0 1.0 copy-start
